TPU v7x, 32 devices: a whole 2x2x4 slice. The times are simulated.
32 devices in a mesh: gp: 32 (over z, y, x, core).
Axes of the slice: x: 2, y: 2, z: 4, core: 2. Of those that a mesh axis runs over, the one named last changes fastest.
Arguments:
- grid_in: bfloat16 [65536, 164], P('gp')
- mesh_static: bfloat16 [65536, 3], P('gp')
- edge_static: bfloat16 [98304, 4], P('gp')
- send_rows: int32 [1024, 64], P('gp')
- edge_src: int32 [98304], P('gp')
- edge_dst: int32 [98304], P('gp')
- w_grid_in: bfloat16 [164, 256], replicated
- w_mesh_in: bfloat16 [3, 256], replicated
- w_edge_in: bfloat16 [4, 256], replicated
- w_edge_up: bfloat16 [768, 256], replicated
- w_mesh_up: bfloat16 [512, 256], replicated
- w_grid_up: bfloat16 [256, 256], replicated
- w_second: bfloat16 [6, 256, 256], replicated
- vectors: float32 [6, 4, 256], replicated
- d_mesh_out: bfloat16 [65536, 256], P('gp')
- d_grid_out: bfloat16 [65536, 256], P('gp')
Outputs:
- output 1: bfloat16 [65536, 256], P('gp')
- output 2: bfloat16 [65536, 256], P('gp')
- output 3: float32 [65536, 164], P('gp')
- output 4: float32 [164, 256], replicated
- output 5: float32 [3, 256], replicated
- output 6: float32 [4, 256], replicated
- output 7: float32 [768, 256], replicated
- output 8: float32 [512, 256], replicated
- output 9: float32 [256, 256], replicated
- output 10: float32 [6, 256, 256], replicated
- output 11: float32 [6, 4, 256], replicated
All inputs are finite; a program needn't handle non-finite values.
Results may differ from a plain program's by a relative error of at most 0.0192591.
Values are sent between devices in bfloat16 or wider.
A program may use at most 1 GiB of HBM per device.

v0:
```python
import jax
import jax.numpy as jnp
from jax import lax
from jax.sharding import PartitionSpec as P

LN_EPS = 1e-5
AXIS_NAME = 'gp'


def matmul(lhs, rhs):
    return jnp.dot(lhs, rhs, preferred_element_type=jnp.float32)


def contract_rows(lhs, rhs):
    return lax.dot_general(lhs, rhs, (((0,), (0,)), ((), ())), preferred_element_type=jnp.float32)


def contract_cols(lhs, rhs):
    return lax.dot_general(lhs, rhs, (((1,), (1,)), ((), ())), preferred_element_type=jnp.float32)


def mlp_tail(pre_act, w_two, vec_rows):
    pre_bias = pre_act + vec_rows[0]
    hidden = jax.nn.silu(pre_bias).astype(jnp.bfloat16)
    out_lin = matmul(hidden, w_two) + vec_rows[1]
    centered = out_lin - jnp.mean(out_lin, axis=-1, keepdims=True)
    inv_std = lax.rsqrt(jnp.mean(centered * centered, axis=-1, keepdims=True) + LN_EPS)
    normed = centered * inv_std
    return normed * vec_rows[2] + vec_rows[3], (pre_bias, hidden, normed, inv_std)


def mlp_tail_back(saved, w_two, vec_rows, d_out):
    pre_bias, hidden, normed, inv_std = saved
    d_normed = d_out * vec_rows[2]
    d_lin = inv_std * (d_normed - jnp.mean(d_normed, axis=-1, keepdims=True) - normed * jnp.mean(d_normed * normed, axis=-1, keepdims=True))
    d_lin_bf = d_lin.astype(jnp.bfloat16)
    d_w_two = contract_rows(hidden, d_lin_bf)
    d_hidden = contract_cols(d_lin_bf, w_two)
    sig_pre = jax.nn.sigmoid(pre_bias)
    d_pre = d_hidden * sig_pre * (1.0 + pre_bias * (1.0 - sig_pre))
    d_vec = jnp.stack([jnp.sum(d_pre, axis=0), jnp.sum(d_lin, axis=0), jnp.sum(d_out * normed, axis=0), jnp.sum(d_out, axis=0)])
    return d_pre.astype(jnp.bfloat16), d_w_two, d_vec


def solution(mesh):
    row_spec = P(AXIS_NAME, None)
    edge_spec = P(AXIS_NAME)
    rep_spec = P()
    in_specs = (row_spec, row_spec, row_spec, row_spec, edge_spec, edge_spec) + (rep_spec,) * 8 + (row_spec, row_spec)
    out_specs = (row_spec, row_spec, row_spec) + (rep_spec,) * 8

    def local_step(grid_in, mesh_static, edge_static, send_rows, edge_src, edge_dst, w_grid_in, w_mesh_in, w_edge_in, w_edge_up, w_mesh_up, w_grid_up, w_second, vectors, d_mesh_out, d_grid_out):
        latent = w_grid_up.shape[0]
        grid_rows = grid_in.shape[0]
        mesh_rows = mesh_static.shape[0]
        slot_rows = send_rows.size
        send_flat = send_rows.reshape(-1)
        up_edge = w_edge_up[:latent]
        up_send = w_edge_up[latent:2 * latent]
        up_recv = w_edge_up[2 * latent:]
        node_self = w_mesh_up[:latent]
        node_agg = w_mesh_up[latent:]

        grid_emb, grid_save = mlp_tail(matmul(grid_in, w_grid_in), w_second[0], vectors[0])
        grid_lat = grid_emb.astype(jnp.bfloat16)
        mesh_emb, mesh_save = mlp_tail(matmul(mesh_static, w_mesh_in), w_second[1], vectors[1])
        mesh_lat = mesh_emb.astype(jnp.bfloat16)
        edge_emb, edge_save = mlp_tail(matmul(edge_static, w_edge_in), w_second[2], vectors[2])
        edge_lat = edge_emb.astype(jnp.bfloat16)

        outgoing = jnp.take(grid_lat, send_flat, axis=0)
        incoming = lax.all_to_all(outgoing, AXIS_NAME, 0, 0, tiled=True)

        edge_pre = (matmul(edge_lat, up_edge)
                    + jnp.take(matmul(incoming, up_send), edge_src, axis=0)
                    + jnp.take(matmul(mesh_lat, up_recv), edge_dst, axis=0))
        edge_upd, upd_save = mlp_tail(edge_pre, w_second[3], vectors[3])
        edge_new = (edge_lat.astype(jnp.float32) + edge_upd).astype(jnp.bfloat16)
        agg_sum = jax.ops.segment_sum(edge_new.astype(jnp.float32), edge_dst, num_segments=mesh_rows).astype(jnp.bfloat16)
        node_upd, node_save = mlp_tail(matmul(mesh_lat, node_self) + matmul(agg_sum, node_agg), w_second[4], vectors[4])
        mesh_out = (mesh_lat.astype(jnp.float32) + node_upd).astype(jnp.bfloat16)
        cell_upd, cell_save = mlp_tail(matmul(grid_lat, w_grid_up), w_second[5], vectors[5])
        grid_out = (grid_lat.astype(jnp.float32) + cell_upd).astype(jnp.bfloat16)

        d_grid_top = d_grid_out.astype(jnp.float32)
        d_mesh_top = d_mesh_out.astype(jnp.float32)
        d_pre5, d_two5, d_vec5 = mlp_tail_back(cell_save, w_second[5], vectors[5], d_grid_top)
        d_w_grid_up = contract_rows(grid_lat, d_pre5)
        d_grid_lat = d_grid_top + contract_cols(d_pre5, w_grid_up)
        d_pre4, d_two4, d_vec4 = mlp_tail_back(node_save, w_second[4], vectors[4], d_mesh_top)
        d_w_mesh_up = jnp.concatenate([contract_rows(mesh_lat, d_pre4), contract_rows(agg_sum, d_pre4)], axis=0)
        d_mesh_lat = d_mesh_top + contract_cols(d_pre4, node_self)
        d_agg = contract_cols(d_pre4, node_agg)
        d_edge_new = jnp.take(d_agg, edge_dst, axis=0)
        d_pre3, d_two3, d_vec3 = mlp_tail_back(upd_save, w_second[3], vectors[3], d_edge_new)
        d_pre3_wide = d_pre3.astype(jnp.float32)
        d_slot_pre = jax.ops.segment_sum(d_pre3_wide, edge_src, num_segments=slot_rows).astype(jnp.bfloat16)
        d_node_pre = jax.ops.segment_sum(d_pre3_wide, edge_dst, num_segments=mesh_rows).astype(jnp.bfloat16)
        d_w_edge_up = jnp.concatenate([contract_rows(edge_lat, d_pre3), contract_rows(incoming, d_slot_pre), contract_rows(mesh_lat, d_node_pre)], axis=0)
        d_edge_lat = d_edge_new + contract_cols(d_pre3, up_edge)
        d_mesh_lat = d_mesh_lat + contract_cols(d_node_pre, up_recv)
        d_incoming = contract_cols(d_slot_pre, up_send).astype(jnp.bfloat16)
        d_outgoing = lax.all_to_all(d_incoming, AXIS_NAME, 0, 0, tiled=True)
        d_grid_lat = d_grid_lat + jax.ops.segment_sum(d_outgoing.astype(jnp.float32), send_flat, num_segments=grid_rows)
        d_pre2, d_two2, d_vec2 = mlp_tail_back(edge_save, w_second[2], vectors[2], d_edge_lat)
        d_w_edge_in = contract_rows(edge_static, d_pre2)
        d_pre1, d_two1, d_vec1 = mlp_tail_back(mesh_save, w_second[1], vectors[1], d_mesh_lat)
        d_w_mesh_in = contract_rows(mesh_static, d_pre1)
        d_pre0, d_two0, d_vec0 = mlp_tail_back(grid_save, w_second[0], vectors[0], d_grid_lat)
        d_w_grid_in = contract_rows(grid_in, d_pre0)
        d_grid_in = contract_cols(d_pre0, w_grid_in)

        weight_grads = (d_w_grid_in, d_w_mesh_in, d_w_edge_in, d_w_edge_up, d_w_mesh_up, d_w_grid_up,
                        jnp.stack([d_two0, d_two1, d_two2, d_two3, d_two4, d_two5]),
                        jnp.stack([d_vec0, d_vec1, d_vec2, d_vec3, d_vec4, d_vec5]))
        weight_grads = lax.psum(weight_grads, AXIS_NAME)
        return (mesh_out, grid_out, d_grid_in) + weight_grads

    return jax.shard_map(local_step, mesh=mesh, in_specs=in_specs, out_specs=out_specs, check_vma=False)
```

profile of v0, /device:TPU:0, one launch (start us, length us, event | category | flops | bytes accessed | tf_op | source)
XLA Modules:
  0.0 459.3 jit_solution(14203352268559909171)
XLA Ops:
  11.8 1.9 fusion.129
  16.0 9.1 %gather_fusion = bf16[2048,256]{1,0:T(8,128)(2,1)} fusion(bf16[2048,256]{1,0:T(8,128)(2,1)S(1)} %copy.38, s32[2048]{0:T(1024)S(1)} %broadcast_clamp_fusion), kind=kCustom, calls=%fused_computation.3 | custom fusion | bytes 2105344 | tf_op jit(solution)/shard_map/jit(_take)/gather | solution.py:71
  25.1 2.4 broadcast_select_fusion
  27.5 7.7 %all-to-all-start = ((bf16[32,64,256]{2,1,0:T(8,128)(2,1)}), bf16[32,64,256]{2,1,0:T(8,128)(2,1)}, u32[]{:S(2)}, u32[]{:S(2)}) async-start(bf16[32,64,256]{2,1,0:T(8,128)(2,1)} %broadcast_select_fusion), calls=%async_computation | async-start | bytes 2097152 | tf_op jit(solution)/shard_map/all_to_all | solution.py:72
  48.9 2.0 fusion.136
  53.7 2.9 copy.44
  57.3 3.9 fusion.128
  63.1 12.4 %gather_fusion.2 = f32[3072,256]{1,0:T(8,128)} fusion(f32[2048,256]{1,0:T(8,128)S(1)} %fusion.95, s32[3072]{0:T(1024)S(1)} %fusion.112), kind=kCustom, calls=%fused_computation.1.clone | custom fusion | bytes 6303744 | tf_op jit(solution)/shard_map/jit(_take)/gather | solution.py:76
  75.5 2.4 multiply_reduce_fusion.5
  81.8 1.9 add_convert_fusion.1
  85.3 12.4 %gather_fusion.1 = f32[3072,256]{1,0:T(8,128)} fusion(f32[2048,256]{1,0:T(8,128)S(1)} %fusion.98, s32[3072]{0:T(1024)S(1)} %fusion.111), kind=kCustom, calls=%fused_computation.clone | custom fusion | bytes 6303744 | tf_op jit(solution)/shard_map/jit(_take)/gather | solution.py:75
  97.7 4.8 %fusion.3 = f32[3072,256]{1,0:T(8,128)S(1)} fusion(bf16[3072,256]{0,1:T(8,128)(2,1)} %add_convert_fusion.1, f32[3072,256]{1,0:T(8,128)} %gather_fusion.2, f32[3072,256]{1,0:T(8,128)} %gather_fusion.1, f32[256]{0:T(256)S(1)} %bitcast.240, pred[3072]{0:T(1024)(128)(4,1)S(1)} %compare_and_fusion.1, pred[3072]{0:T(1024)(128)(4,1)S(1)} %compare_and_fusion.2, ...), kind=kOutput, calls=%fused_computation.16 | convolution fusion | flops 406585344 | bytes 11148288 | tf_op jit(solution)/shard_map/dot_general | solution.py:11
  102.5 2.3 fusion.130
  107.9 3.0 fusion.29
  110.9 3.6 copy.39
  114.5 17.9 %scatter_custom_fusion = f32[2048,256]{1,0:T(8,128)S(1)} fusion(s32[3072]{0:T(1024)} %param.23, f32[3072,256]{1,0:T(8,128)} %copy.39, f32[]{:T(128)} %constant.63.clone.1), kind=kCustom, calls=%fused_computation.134 | custom fusion | flops 786432 | bytes 2097664 | tf_op jit(solution)/shard_map/scatter-add | solution.py:79
  132.4 2.0 fusion.18
  134.5 1.9 fusion.131
  139.1 3.0 fusion.124
  146.7 12.6 %gather_fusion.3 = f32[3072,256]{1,0:T(8,128)} fusion(f32[2048,256]{1,0:T(8,128)S(1)} %fusion.89, s32[3072]{0:T(1024)S(1)} %fusion.112), kind=kCustom, calls=%fused_computation.2.clone | custom fusion | bytes 6303744 | tf_op jit(solution)/shard_map/jit(_take)/gather | solution.py:94
  159.3 3.5 copy.43
  162.8 5.4 %multiply_reduce_fusion = (f32[256]{0:T(256)}, f32[3072]{0:T(1024)S(1)}, f32[3072]{0:T(1024)S(1)}, f32[256]{0:T(256)}) fusion(f32[3072,256]{0,1:T(8,128)} %copy.43, f32[3072,256]{0,1:T(8,128)} %copy-done.8, f32[3072]{0:T(1024)S(1)} %add_rsqrt_fusion, f32[3072]{0:T(1024)S(1)} %broadcast_multiply_fusion.4, pred[3072]{0:T(1024)(128)(4,1)S(1)} %compare_and_fusion.1, ...), kind=kLoop, calls=%fused_computation.31 | loop fusion | flops 7857664 | bytes 6346752 | tf_op jit(solution)/shard_map/reduce_sum | solution.py:41
  168.3 2.2 fusion.119
  170.5 3.2 fusion.123
  175.6 3.9 multiply_reduce_fusion.1
  179.5 18.7 %scatter_custom_fusion.3 = f32[2048,256]{1,0:T(8,128)} fusion(s32[3072]{0:T(1024)} %param.23, bf16[3072,256]{1,0:T(8,128)(2,1)S(1)} %get-tuple-element.76, f32[]{:T(128)} %constant.63.clone.1), kind=kCustom, calls=%fused_computation.19 | custom fusion | flops 1572864 | bytes 3670528 | tf_op jit(solution)/shard_map/scatter-add | solution.py:98
  198.2 18.9 %scatter_custom_fusion.1 = f32[2048,256]{1,0:T(8,128)} fusion(s32[3072]{0:T(1024)} %param.22, bf16[3072,256]{1,0:T(8,128)(2,1)S(1)} %get-tuple-element.76, f32[]{:T(128)} %constant.63.clone.1), kind=kCustom, calls=%fused_computation.21 | custom fusion | flops 1572864 | bytes 3670528 | tf_op jit(solution)/shard_map/scatter-add | solution.py:97
  217.0 3.2 fusion.60
  224.3 4.5 multiply_reduce_fusion.8
  228.9 6.1 %all-to-all-start.1 = ((bf16[32,64,256]{2,1,0:T(8,128)(2,1)}), bf16[32,64,256]{2,1,0:T(8,128)(2,1)}, u32[]{:S(2)}, u32[]{:S(2)}) async-start(bf16[32,64,256]{2,1,0:T(8,128)(2,1)} %bitcast.204), calls=%async_computation.1 | async-start | bytes 2097152 | tf_op jit(solution)/shard_map/all_to_all | solution.py:103
  235.2 7.5 %fusion.114 = (f32[256]{0:T(256)}, f32[256]{0:T(256)}, f32[256]{0:T(256)}, bf16[2048,256]{0,1:T(8,128)(2,1)}, bf16[2048,256]{0,1:T(8,128)(2,1)}, /*index=5*/f32[256]{0:T(256)}, f32[256]{0:T(256)}, f32[256]{0:T(256)}) fusion(f32[2048]{0:T(1024)S(1)} %copy-done.80, f32[2048,256]{0,1:T(8,128)} %copy-done.17, f32[2048]{0:T(1024)S(1)} %broadcast_multiply_fusion.14, ...), kind=kLoop, calls=%fused_computation.250 | loop fusion | flops 23067136 | bytes 12695552 | tf_op jit(solution)/shard_map/reduce_sum | solution.py:41
  243.5 2.3 copy.51
  245.8 2.3 copy.50
  248.1 1.9 pad_maximum_fusion
  250.0 4.3 fusion.120
  254.3 2.6 fusion.135
  257.2 3.8 all-to-all-done.1
  261.0 14.9 %scatter_custom_fusion.2 = f32[2048,256]{1,0:T(8,128)} fusion(f32[2048,256]{1,0:T(8,128)} %copy.44, s32[2048]{0:T(1024)} %reshape.295, bf16[2048,256]{1,0:T(8,128)(2,1)} %bitcast.74), kind=kCustom, calls=%fused_computation.83 | custom fusion | flops 1048576 | bytes 3145728 | tf_op jit(solution)/shard_map/scatter-add | solution.py:104
  275.9 1.9 reduce_sum.459
  277.8 3.2 copy.45
  280.9 3.3 multiply_reduce_fusion.9
  284.4 3.2 fusion.121
  287.6 2.1 fusion.133
  303.8 3.0 fusion.134
  307.4 40.3 %all-reduce = (f32[3,256]{1,0:T(4,128)}, f32[4,256]{1,0:T(4,128)}, f32[6,4,256]{2,1,0:T(4,128)}) all-reduce(f32[3,256]{1,0:T(4,128)S(1)} %convolution_bitcast_fusion.7, f32[4,256]{1,0:T(4,128)S(1)} %fusion.38, f32[6,4,256]{2,1,0:T(4,128)S(1)} %constant_dynamic-update-slice_fusion), channel_id=1, replica_groups=mesh['gp'=32] {'gp'}, use_global_device_ids=true, to_apply=%region_27.29 | all-reduce | flops 7936 | bytes 63488 | tf_op jit(solution)/shard_map/psum | solution.py:116
  349.2 95.3 %all-reduce.4.cloned.1.call-done = (f32[164,256]{1,0:T(8,128)}, f32[768,256]{1,0:T(8,128)}, f32[512,256]{1,0:T(8,128)}, f32[256,256]{1,0:T(8,128)}, f32[6,256,256]{2,1,0:T(8,128)}) async-done(((f32[164,256]{1,0:T(8,128)}, f32[768,256]{1,0:T(8,128)}, f32[512,256]{1,0:T(8,128)}, f32[256,256]{1,0:T(8,128)}, f32[6,256,256]{2,1,0:T(8,128)}), (f32[164,256]{1,0:T(8,128)}, f32[768,256]{1,0:T(8,128)}, ...) | async-done | bytes 3313680 | tf_op jit(solution)/shard_map/psum | solution.py:116
  446.3 2.1 copy.73
  448.3 1.9 copy.74
  (353 shorter events, 67.9 us)
Async XLA Ops:
  10.3 3.7 copy-start.92
  10.3 3.7 copy-start.101
  10.4 38.5 %copy-start.96 = (f32[1,1,256]{2,1,0:T(1,128)}, f32[1,1,256]{2,1,0:T(1,128)S(1)}, u32[]{:S(2)}) copy-start(f32[1,1,256]{2,1,0:T(1,128)S(1)} %get-tuple-element.81) | copy-start | bytes 3076
  15.4 9.6 %copy-start.22 = (bf16[2048,256]{0,1:T(8,128)(2,1)}, bf16[2048,256]{0,1:T(8,128)(2,1)S(1)}, u32[]{:S(2)}) copy-start(bf16[2048,256]{0,1:T(8,128)(2,1)S(1)} %add_convert_fusion.4) | copy-start | bytes 3145732
  25.0 11.5 %copy-start.63 = (s32[32,64]{1,0:T(8,128)S(1)}, s32[32,64]{1,0:T(8,128)}, u32[]{:S(2)}) copy-start(s32[32,64]{1,0:T(8,128)} %param.21) | copy-start | bytes 24580
  25.0 12.2 %copy-start.73 = (s32[3072]{0:T(1024)S(1)}, s32[3072]{0:T(1024)}, u32[]{:S(2)}) copy-start(s32[3072]{0:T(1024)} %param.23) | copy-start | bytes 36868
  25.1 12.2 %copy-start.74 = (s32[3072]{0:T(1024)S(1)}, s32[3072]{0:T(1024)}, u32[]{:S(2)}) copy-start(s32[3072]{0:T(1024)} %param.22) | copy-start | bytes 36868
  25.1 12.3 %copy-start.55 = (bf16[2048,256]{1,0:T(8,128)(2,1)S(1)}, bf16[2048,256]{1,0:T(8,128)(2,1)}, u32[]{:S(2)}) copy-start(bf16[2048,256]{1,0:T(8,128)(2,1)} %param.32) | copy-start | bytes 3145732
  27.5 11.3 %copy-start.56 = (bf16[2048,256]{1,0:T(8,128)(2,1)S(1)}, bf16[2048,256]{1,0:T(8,128)(2,1)}, u32[]{:S(2)}) copy-start(bf16[2048,256]{1,0:T(8,128)(2,1)} %param.33) | copy-start | bytes 3145732
  27.5 56.2 %all-to-all-start = ((bf16[32,64,256]{2,1,0:T(8,128)(2,1)}), bf16[32,64,256]{2,1,0:T(8,128)(2,1)}, u32[]{:S(2)}, u32[]{:S(2)}) async-start(bf16[32,64,256]{2,1,0:T(8,128)(2,1)} %broadcast_select_fusion), calls=%async_computation | async-start | bytes 2097152 | tf_op jit(solution)/shard_map/all_to_all | solution.py:72
  36.6 24.6 %copy-start.88 = (f32[1,1,256]{2,1,0:T(1,128)}, f32[1,1,256]{2,1,0:T(1,128)S(1)}, u32[]{:S(2)}) copy-start(f32[1,1,256]{2,1,0:T(1,128)S(1)} %get-tuple-element.102) | copy-start | bytes 3076
  36.6 24.6 %copy-start.103 = (f32[1,1,256]{2,1,0:T(1,128)}, f32[1,1,256]{2,1,0:T(1,128)S(1)}, u32[]{:S(2)}) copy-start(f32[1,1,256]{2,1,0:T(1,128)S(1)} %get-tuple-element.101) | copy-start | bytes 3076
  42.9 18.4 %copy-start.4 = (f32[2048,256]{0,1:T(8,128)}, f32[2048,256]{0,1:T(8,128)S(1)}, u32[]{:S(2)}) copy-start(f32[2048,256]{0,1:T(8,128)S(1)} %get-tuple-element.106) | copy-start | bytes 6291460
  46.5 4.4 copy-start.66
  57.2 4.0 copy-start.32
  75.5 3.6 copy-start.12
  75.5 3.6 copy-start.54
  85.3 12.4 %copy-start.110 = (f32[1,1,256]{2,1,0:T(1,128)S(1)}, f32[1,1,256]{2,1,0:T(1,128)}, u32[]{:S(2)}) copy-start(f32[1,1,256]{2,1,0:T(1,128)} %get-tuple-element.91) | copy-start | bytes 3076
  97.7 4.9 %copy-start.128 = (f32[1,1,256]{2,1,0:T(1,128)S(1)}, f32[1,1,256]{2,1,0:T(1,128)}, u32[]{:S(2)}) copy-start(f32[1,1,256]{2,1,0:T(1,128)} %get-tuple-element.90) | copy-start | bytes 3076
  114.5 17.9 %copy-start.123 = (f32[1,1,256]{2,1,0:T(1,128)S(1)}, f32[1,1,256]{2,1,0:T(1,128)}, u32[]{:S(2)}) copy-start(f32[1,1,256]{2,1,0:T(1,128)} %get-tuple-element.87) | copy-start | bytes 3076
  134.5 4.6 copy-start.44
  136.7 5.3 %copy-start.68 = (f32[2048]{0:T(1024)}, f32[2048]{0:T(1024)S(1)}, u32[]{:S(2)}) copy-start(f32[2048]{0:T(1024)S(1)} %add_rsqrt_fusion.3) | copy-start | bytes 24580
  162.8 5.4 %copy-start.9 = (f32[3072,256]{0,1:T(8,128)S(1)}, f32[3072,256]{0,1:T(8,128)}, u32[]{:S(2)}) copy-start(f32[3072,256]{0,1:T(8,128)} %copy-done.8) | copy-start | bytes 9437188
  162.8 5.5 %copy-start.10 = (f32[3072,256]{0,1:T(8,128)S(1)}, f32[3072,256]{0,1:T(8,128)}, u32[]{:S(2)}) copy-start(f32[3072,256]{0,1:T(8,128)} %copy.43) | copy-start | bytes 9437188
  228.8 6.2 %copy-start.67 = (f32[2048]{0:T(1024)S(1)}, f32[2048]{0:T(1024)}, u32[]{:S(2)}) copy-start(f32[2048]{0:T(1024)} %copy-done.66) | copy-start | bytes 24580
  228.8 6.3 %copy-start.69 = (f32[2048]{0:T(1024)S(1)}, f32[2048]{0:T(1024)}, u32[]{:S(2)}) copy-start(f32[2048]{0:T(1024)} %copy-done.68) | copy-start | bytes 24580
  228.8 6.3 %copy-start.77 = (f32[2048]{0:T(1024)S(1)}, f32[2048]{0:T(1024)}, u32[]{:S(2)}) copy-start(f32[2048]{0:T(1024)} %copy-done.76) | copy-start | bytes 24580
  228.8 6.3 %copy-start.80 = (f32[2048]{0:T(1024)S(1)}, f32[2048]{0:T(1024)}, u32[]{:S(2)}) copy-start(f32[2048]{0:T(1024)} %copy-done.79) | copy-start | bytes 24580
  228.8 6.3 %copy-start.83 = (f32[2048]{0:T(1024)S(1)}, f32[2048]{0:T(1024)}, u32[]{:S(2)}) copy-start(f32[2048]{0:T(1024)} %copy-done.82) | copy-start | bytes 24580
  228.8 6.3 %copy-start.86 = (f32[2048]{0:T(1024)S(1)}, f32[2048]{0:T(1024)}, u32[]{:S(2)}) copy-start(f32[2048]{0:T(1024)} %copy-done.85) | copy-start | bytes 24580
  228.8 6.3 %copy-start.93 = (f32[1,1,256]{2,1,0:T(1,128)S(1)}, f32[1,1,256]{2,1,0:T(1,128)}, u32[]{:S(2)}) copy-start(f32[1,1,256]{2,1,0:T(1,128)} %copy-done.92) | copy-start | bytes 3076
  228.8 6.3 %copy-start.97 = (f32[1,1,256]{2,1,0:T(1,128)S(1)}, f32[1,1,256]{2,1,0:T(1,128)}, u32[]{:S(2)}) copy-start(f32[1,1,256]{2,1,0:T(1,128)} %copy-done.96) | copy-start | bytes 3076
  228.8 6.3 %copy-start.99 = (f32[1,1,256]{2,1,0:T(1,128)S(1)}, f32[1,1,256]{2,1,0:T(1,128)}, u32[]{:S(2)}) copy-start(f32[1,1,256]{2,1,0:T(1,128)} %get-tuple-element.85) | copy-start | bytes 3076
  228.8 6.3 %copy-start.102 = (f32[1,1,256]{2,1,0:T(1,128)S(1)}, f32[1,1,256]{2,1,0:T(1,128)}, u32[]{:S(2)}) copy-start(f32[1,1,256]{2,1,0:T(1,128)} %copy-done.101) | copy-start | bytes 3076
  228.8 6.3 %copy-start.104 = (f32[1,1,256]{2,1,0:T(1,128)S(1)}, f32[1,1,256]{2,1,0:T(1,128)}, u32[]{:S(2)}) copy-start(f32[1,1,256]{2,1,0:T(1,128)} %copy-done.103) | copy-start | bytes 3076
  228.8 6.3 %copy-start.107 = (f32[1,1,256]{2,1,0:T(1,128)S(1)}, f32[1,1,256]{2,1,0:T(1,128)}, u32[]{:S(2)}) copy-start(f32[1,1,256]{2,1,0:T(1,128)} %get-tuple-element.84) | copy-start | bytes 3076
  228.8 6.3 %copy-start.108 = (f32[1,1,256]{2,1,0:T(1,128)S(1)}, f32[1,1,256]{2,1,0:T(1,128)}, u32[]{:S(2)}) copy-start(f32[1,1,256]{2,1,0:T(1,128)} %get-tuple-element.100) | copy-start | bytes 3076
  228.9 32.1 %all-to-all-start.1 = ((bf16[32,64,256]{2,1,0:T(8,128)(2,1)}), bf16[32,64,256]{2,1,0:T(8,128)(2,1)}, u32[]{:S(2)}, u32[]{:S(2)}) async-start(bf16[32,64,256]{2,1,0:T(8,128)(2,1)} %bitcast.204), calls=%async_computation.1 | async-start | bytes 2097152 | tf_op jit(solution)/shard_map/all_to_all | solution.py:103
  235.0 209.6 %all-reduce.4.cloned.1.call-start = ((), (), s32[]{:S(2)}) async-start(), calls=%async_computation.2 | async-start | bytes 6635520 | tf_op jit(solution)/shard_map/psum | solution.py:116
  235.1 7.5 %copy-start.57 = (f32[256,256]{1,0:T(8,128)S(1)}, f32[256,256]{1,0:T(8,128)}, u32[]{:S(2)}) copy-start(f32[256,256]{1,0:T(8,128)} %fusion.138) | copy-start | bytes 786436
  235.2 7.5 %copy-start.58 = (f32[256,256]{1,0:T(8,128)S(1)}, f32[256,256]{1,0:T(8,128)}, u32[]{:S(2)}) copy-start(f32[256,256]{1,0:T(8,128)} %fusion.70) | copy-start | bytes 786436
  243.5 4.6 %copy-start.59 = (f32[256,256]{1,0:T(8,128)S(1)}, f32[256,256]{1,0:T(8,128)}, u32[]{:S(2)}) copy-start(f32[256,256]{1,0:T(8,128)} %fusion.60) | copy-start | bytes 786436
  245.8 4.2 copy-start.75
  245.8 4.2 copy-start.72
  250.0 4.3 copy-start.33
  303.8 43.8 %copy-start.61 = (bf16[164,256]{1,0:T(8,128)(2,1)S(1)}, bf16[164,256]{1,0:T(8,128)(2,1)}, u32[]{:S(2)}) copy-start(bf16[164,256]{1,0:T(8,128)(2,1)} %param.24) | copy-start | bytes 251908
  444.5 5.7 %copy-start.62 = (f32[256,256]{1,0:T(8,128)S(1)}, f32[256,256]{1,0:T(8,128)}, u32[]{:S(2)}) copy-start(f32[256,256]{1,0:T(8,128)} %get-tuple-element.161) | copy-start | bytes 786436
  444.5 6.4 %copy-start.47 = (f32[6,256,256]{2,1,0:T(8,128)S(1)}, f32[6,256,256]{2,1,0:T(8,128)}, u32[]{:S(2)}) copy-start(f32[6,256,256]{2,1,0:T(8,128)} %get-tuple-element.162) | copy-start | bytes 4718596
  (88 other events, 221.0 us)
Sparse Core Ops, SparseCore 0:
  303.8 140.7 all-reduce.3
where the time goes:
time: 464 us; the launch traced here: 459 us
  other arithmetic  115 us (25%)
  local copies, waits for them, and re-layouts  101 us (22%)
  waiting for transfers between devices  99.2 us (21%)
  matrix products  73.9 us (16%)
  blocking collectives  40.3 us (9%)
  between operations  16.1 us (3%)
  starting transfers between devices  13.8 us (3%)
    psum x1, waiting for transfers between devices, local_step(): weight_grads = lax.psum(weight_grads, AXIS_NAME)  95.3 us
    psum x1, blocking collectives, local_step(): weight_grads = lax.psum(weight_grads, AXIS_NAME)  40.3 us
    unnamed x275, local copies, waits for them, and re-layouts  37 us
    dot_general x13, matrix products, contract_cols(): lax.dot_general(lhs, rhs, (((1,), (1,)), ((), ())), preferred_element_typ...  31.4 us
    dot_general x15, matrix products, matmul(): return jnp.dot(lhs, rhs, preferred_element_type=jnp.float32)  25.6 us
    scatter-add x1, other arithmetic, local_step(): jax.ops.segment_sum(d_pre3_wide, edge_src, num_segments=slot_rows)  18.9 us
    scatter-add x1, other arithmetic, local_step(): jax.ops.segment_sum(d_pre3_wide, edge_dst, num_segments=mesh_rows)  18.7 us
    scatter-add x1, other arithmetic, local_step(): jax.ops.segment_sum(edge_new.astype(jnp.float32), edge_dst, num_segments=...  17.9 us
  transfers between devices with their start and end apart: 3, of which 2 were waited for; matrix products, arithmetic and copies ran while one was open for 15% of the time, Pallas kernels for 0%

commit v1 on v0

v1 whole, which is shorter than its diff:
```python
import functools

import jax
import jax.numpy as jnp
from jax import lax
from jax.experimental import pallas as pl
from jax.experimental.pallas import tpu as pltpu
from jax.sharding import PartitionSpec as P

LN_EPS = 1e-5
AXIS = 'gp'
BF = jnp.bfloat16
F32 = jnp.float32
MESH = pl.DeviceIdType.MESH
TILE = 256
VMEM_LIMIT = 60 * 1024 * 1024


def nn(lhs, rhs):
    return jnp.dot(lhs, rhs, preferred_element_type=F32)


def tn(lhs, rhs):
    return lax.dot_general(lhs, rhs, (((0,), (0,)), ((), ())), preferred_element_type=F32)


def nt(lhs, rhs):
    return lax.dot_general(lhs, rhs, (((1,), (1,)), ((), ())), preferred_element_type=F32)


def mlp_fwd(pre_act, w_two, vec):
    act = pre_act + vec[0:1]
    sig = 0.5 * jnp.tanh(0.5 * act) + 0.5
    hidden = (act * sig).astype(BF)
    lin = nn(hidden, w_two) + vec[1:2]
    cen = lin - jnp.mean(lin, axis=-1, keepdims=True)
    inv = lax.rsqrt(jnp.mean(cen * cen, axis=-1, keepdims=True) + LN_EPS)
    normed = cen * inv
    return (act, sig, hidden, normed, inv), normed * vec[2:3] + vec[3:4]


def mlp_bwd(saved, w_two, vec, d_out):
    act, sig, hidden, normed, inv = saved
    d_n = d_out * vec[2:3]
    m_one = jnp.mean(d_n, axis=-1, keepdims=True)
    m_two = jnp.mean(d_n * normed, axis=-1, keepdims=True)
    d_lin = inv * (d_n - m_one - normed * m_two)
    d_lin_bf = d_lin.astype(BF)
    d_two = tn(hidden, d_lin_bf)
    d_hid = nt(d_lin_bf, w_two)
    d_pre = d_hid * (sig * (1.0 + act * (1.0 - sig)))
    d_vec = [jnp.sum(d_pre, axis=0, keepdims=True), jnp.sum(d_lin, axis=0, keepdims=True),
             jnp.sum(d_out * normed, axis=0, keepdims=True), jnp.sum(d_out, axis=0, keepdims=True)]
    return d_pre.astype(BF), d_two, d_vec


def add_vec(ref, base, d_vec):
    for j in range(4):
        ref[base + j:base + j + 1, :] += d_vec[j]


def rows_at(i, size=TILE):
    return pl.ds(pl.multiple_of(i * size, size), size)


def hot_cols(col_idx, width):
    ids = lax.broadcasted_iota(jnp.int32, (col_idx.shape[0], width), 1)
    return jnp.where(ids == col_idx, 1.0, 0.0).astype(BF)


def hot_rows(row_idx, base, height):
    ids = lax.broadcasted_iota(jnp.int32, (height, row_idx.shape[1]), 0) + base
    return jnp.where(ids == row_idx, 1.0, 0.0).astype(BF)


def loop(n, body):
    def step(i, carry):
        body(i)
        return carry
    lax.fori_loop(0, n, step, 0)


def grid_fwd_kernel(grid_t, send_col, w_grid_in, w_two, vec, lat_out, send_out):
    def embed(i):
        sl = rows_at(i)
        _, emb = mlp_fwd(tn(grid_t[:, sl], w_grid_in[...]), w_two[0], vec[0])
        lat_out[sl, :] = emb.astype(BF)
    loop(lat_out.shape[0] // TILE, embed)

    def pick(i):
        sl = rows_at(i)
        send_out[sl, :] = nn(hot_cols(send_col[sl, :], lat_out.shape[0]), lat_out[...]).astype(BF)
    loop(send_out.shape[0] // TILE, pick)


def local_kernel(grid_lat, d_grid, mesh_t, edge_t, dst_col, w_mesh_in, w_edge_in, w_edge_up, w_grid_up, w_two, vec,
                 grid_out, d_lat_out, mesh_lat, edge_lat, recv_lat, grad):
    lat = w_grid_up.shape[0]
    grad[...] = jnp.zeros_like(grad)

    def cells(i):
        sl = rows_at(i)
        here = grid_lat[sl, :]
        saved, upd = mlp_fwd(nn(here, w_grid_up[...]), w_two[5], vec[5])
        grid_out[sl, :] = (here.astype(F32) + upd).astype(BF)
        d_top = d_grid[sl, :].astype(F32)
        d_pre, d_two, d_vec = mlp_bwd(saved, w_two[5], vec[5], d_top)
        grad[0:lat, :] += tn(here, d_pre)
        grad[lat:2 * lat, :] += d_two
        add_vec(grad, 2 * lat, d_vec)
        d_lat_out[sl, :] = d_top + nt(d_pre, w_grid_up[...])
    loop(grid_lat.shape[0] // TILE, cells)

    def nodes(i):
        sl = rows_at(i)
        _, emb = mlp_fwd(tn(mesh_t[:, sl], w_mesh_in[...]), w_two[1], vec[1])
        mesh_lat[sl, :] = emb.astype(BF)
    loop(mesh_lat.shape[0] // TILE, nodes)

    def edges(i):
        sl = rows_at(i)
        _, emb = mlp_fwd(tn(edge_t[:, sl], w_edge_in[...]), w_two[2], vec[2])
        edge_lat[sl, :] = emb.astype(BF)
        recv_lat[sl, :] = nn(hot_cols(dst_col[sl, :], mesh_lat.shape[0]), mesh_lat[...]).astype(BF)
    loop(edge_lat.shape[0] // TILE, edges)


def edge_kernel(incoming, mesh_lat, edge_lat, recv_lat, d_mesh, src_col, dst_col, src_row, dst_row, w_edge_up, w_mesh_up, w_two, vec,
                mesh_out, d_mesh_lat, d_edge_lat, d_pre3, d_incoming, grad,
                send_lat, edge_new, act_s, nrm_s, inv_s, d_pre4):
    lat = 256
    n_edge, n_mesh, n_slot = edge_lat.shape[0], mesh_lat.shape[0], incoming.shape[0]
    o_mesh, o_edge, o_four, o_three, o_vec = 0, 2 * lat, 5 * lat, 6 * lat, 7 * lat
    grad[...] = jnp.zeros_like(grad)

    def edges_fwd(i):
        sl = rows_at(i)
        sent = nn(hot_cols(src_col[sl, :], n_slot), incoming[...]).astype(BF)
        send_lat[sl, :] = sent
        here = edge_lat[sl, :]
        pre = nn(here, w_edge_up[0:lat, :]) + nn(sent, w_edge_up[lat:2 * lat, :]) + nn(recv_lat[sl, :], w_edge_up[2 * lat:3 * lat, :])
        (act, _, _, normed, inv), upd = mlp_fwd(pre, w_two[3], vec[3])
        act_s[sl, :] = act
        nrm_s[sl, :] = normed
        inv_s[sl, :] = jnp.broadcast_to(inv, (TILE, 128))
        edge_new[sl, :] = (here.astype(F32) + upd).astype(BF)
    loop(n_edge // TILE, edges_fwd)

    def nodes(i):
        sl = rows_at(i)
        agg = nn(hot_rows(dst_row[...], i * TILE, TILE), edge_new[...]).astype(BF)
        here = mesh_lat[sl, :]
        saved, upd = mlp_fwd(nn(here, w_mesh_up[0:lat, :]) + nn(agg, w_mesh_up[lat:2 * lat, :]), w_two[4], vec[4])
        mesh_out[sl, :] = (here.astype(F32) + upd).astype(BF)
        d_top = d_mesh[sl, :].astype(F32)
        d_pre, d_two, d_vec = mlp_bwd(saved, w_two[4], vec[4], d_top)
        d_pre4[sl, :] = d_pre
        grad[o_mesh:o_mesh + lat, :] += tn(here, d_pre)
        grad[o_mesh + lat:o_mesh + 2 * lat, :] += tn(agg, d_pre)
        grad[o_four:o_four + lat, :] += d_two
        add_vec(grad, o_vec, d_vec)
        d_mesh_lat[sl, :] = d_top + nt(d_pre, w_mesh_up[0:lat, :])
    loop(n_mesh // TILE, nodes)

    def edges_bwd(i):
        sl = rows_at(i)
        picked = nn(hot_cols(dst_col[sl, :], n_mesh), d_pre4[...]).astype(BF)
        d_new = nt(picked, w_mesh_up[lat:2 * lat, :])
        act = act_s[sl, :]
        sig = 0.5 * jnp.tanh(0.5 * act) + 0.5
        hidden = (act * sig).astype(BF)
        d_pre, d_two, d_vec = mlp_bwd((act, sig, hidden, nrm_s[sl, :], inv_s[sl, 0:1]), w_two[3], vec[3], d_new)
        d_pre3[sl, :] = d_pre
        grad[o_three:o_three + lat, :] += d_two
        add_vec(grad, o_vec + 4, d_vec)
        grad[o_edge:o_edge + lat, :] += tn(edge_lat[sl, :], d_pre)
        grad[o_edge + lat:o_edge + 2 * lat, :] += tn(send_lat[sl, :], d_pre)
        grad[o_edge + 2 * lat:o_edge + 3 * lat, :] += tn(recv_lat[sl, :], d_pre)
        d_edge_lat[sl, :] = d_new + nt(d_pre, w_edge_up[0:lat, :])
    loop(n_edge // TILE, edges_bwd)

    def slots(i):
        sl = rows_at(i)
        d_slot = nn(hot_rows(src_row[...], i * TILE, TILE), d_pre3[...]).astype(BF)
        d_incoming[sl, :] = nt(d_slot, w_edge_up[lat:2 * lat, :]).astype(BF)
    loop(n_slot // TILE, slots)


def embed_bwd_kernel(mesh_t, edge_t, dst_row, d_pre3, d_mesh_lat, d_edge_lat, w_mesh_in, w_edge_in, w_edge_up, w_two, vec, grad):
    lat = 256
    grad[...] = jnp.zeros_like(grad)
    o_vec = 2 * lat + 16

    def nodes(i):
        sl = rows_at(i)
        d_node = nn(hot_rows(dst_row[...], i * TILE, TILE), d_pre3[...]).astype(BF)
        d_top = d_mesh_lat[sl, :] + nt(d_node, w_edge_up[2 * lat:3 * lat, :])
        feat = mesh_t[:, sl]
        saved, _ = mlp_fwd(tn(feat, w_mesh_in[...]), w_two[1], vec[1])
        d_pre, d_two, d_vec = mlp_bwd(saved, w_two[1], vec[1], d_top)
        grad[0:lat, :] += d_two
        grad[2 * lat:2 * lat + 3, :] += nn(feat, d_pre)
        add_vec(grad, o_vec, d_vec)
    loop(d_mesh_lat.shape[0] // TILE, nodes)

    def edges(i):
        sl = rows_at(i)
        feat = edge_t[:, sl]
        saved, _ = mlp_fwd(tn(feat, w_edge_in[...]), w_two[2], vec[2])
        d_pre, d_two, d_vec = mlp_bwd(saved, w_two[2], vec[2], d_edge_lat[sl, :])
        grad[lat:2 * lat, :] += d_two
        grad[2 * lat + 8:2 * lat + 12, :] += nn(feat, d_pre)
        add_vec(grad, o_vec + 4, d_vec)
    loop(d_edge_lat.shape[0] // TILE, edges)


def grid_bwd_kernel(grid_t, send_row, d_sent, d_lat, w_grid_in, w_two, vec, d_grid_t, grad):
    feat_n = grid_t.shape[0]
    lat = 256
    grad[...] = jnp.zeros_like(grad)

    def body(i):
        sl = rows_at(i)
        d_top = d_lat[sl, :] + nn(hot_rows(send_row[...], i * TILE, TILE), d_sent[...])
        feat = grid_t[:, sl]
        saved, _ = mlp_fwd(tn(feat, w_grid_in[...]), w_two[0], vec[0])
        d_pre, d_two, d_vec = mlp_bwd(saved, w_two[0], vec[0], d_top)
        grad[0:lat, :] += d_two
        grad[lat:lat + feat_n, :] += nn(feat, d_pre)
        add_vec(grad, lat + 168, d_vec)
        d_grid_t[:, sl] = nt(w_grid_in[...], d_pre)
    loop(d_lat.shape[0] // TILE, body)


def sum_kernel(parts, g_a, g_b, g_c, g_d, out, own, r_one, r_two, r_three, r_four, send_sem, recv_sem, z_send, z_recv):
    me = lax.axis_index(AXIS)
    core = lax.rem(me, 2)
    x_at = lax.rem(me // 2, 2)
    y_at = lax.rem(me // 4, 2)
    z_at = me // 8
    piece = out.shape[0] // 32
    swap_x = me + 2 * (1 - 2 * x_at)
    swap_y = me + 4 * (1 - 2 * y_at)
    swap_c = me + 1 - 2 * core
    first = (1 - core) * swap_x + core * swap_y
    second = (1 - core) * swap_y + core * swap_x
    bit_one = (1 - core) * x_at + core * y_at
    bit_two = (1 - core) * y_at + core * x_at
    plane = me - 8 * z_at

    barrier = pltpu.get_barrier_semaphore()
    pl.semaphore_signal(barrier, inc=1, device_id=(swap_x,), device_id_type=MESH)
    pl.semaphore_signal(barrier, inc=1, device_id=(swap_y,), device_id_type=MESH)
    pl.semaphore_signal(barrier, inc=1, device_id=(swap_c,), device_id_type=MESH)
    for k in range(1, 4):
        pl.semaphore_signal(barrier, inc=1, device_id=(plane + 8 * lax.rem(z_at + k, 4),), device_id_type=MESH)

    base = 0
    for g in (g_a, g_b, g_c, g_d):
        own[base:base + g.shape[0], :] = g[...]
        base += g.shape[0]
    if base < own.shape[0]:
        own[base:, :] = jnp.zeros((own.shape[0] - base, own.shape[1]), F32)
    pl.semaphore_wait(barrier, 6)

    def at(start, size):
        return pl.ds(pl.multiple_of(start, 8), size)

    def exchange(k, src, dst, peer):
        copy = pltpu.make_async_remote_copy(src_ref=src, dst_ref=dst, send_sem=send_sem.at[k], recv_sem=recv_sem.at[k], device_id=(peer,), device_id_type=MESH)
        copy.start()
        copy.wait()

    half, quarter, eighth = 16 * piece, 8 * piece, 4 * piece
    lo_one = core * half
    exchange(0, own.at[at((1 - core) * half, half)], r_one, swap_c)
    own[at(lo_one, half), :] += r_one[...]
    lo_two = lo_one + bit_one * quarter
    exchange(1, own.at[at(lo_one + (1 - bit_one) * quarter, quarter)], r_two, first)
    own[at(lo_two, quarter), :] += r_two[...]
    lo_three = lo_two + bit_two * eighth
    exchange(2, own.at[at(lo_two + (1 - bit_two) * eighth, eighth)], r_three, second)
    own[at(lo_three, eighth), :] += r_three[...]

    copies = []
    for k in range(1, 4):
        z_to = lax.rem(z_at + k, 4)
        copies.append(pltpu.make_async_remote_copy(
            src_ref=own.at[at(lo_three + z_to * piece, piece)], dst_ref=r_four.at[k - 1],
            send_sem=z_send.at[k - 1], recv_sem=z_recv.at[k - 1], device_id=(plane + 8 * z_to,), device_id_type=MESH))
    for copy in copies:
        copy.start()
    for copy in copies:
        copy.wait()
    lo_four = lo_three + z_at * piece
    out[at(lo_four, piece), :] = own[at(lo_four, piece), :] + (r_four[0] + r_four[1] + r_four[2])

    copies = []
    for k in range(1, 4):
        z_to = lax.rem(z_at + k, 4)
        copies.append(pltpu.make_async_remote_copy(
            src_ref=out.at[at(lo_four, piece)], dst_ref=out.at[at(lo_four, piece)],
            send_sem=z_send.at[k + 2], recv_sem=z_recv.at[k + 2], device_id=(plane + 8 * z_to,), device_id_type=MESH))
    for copy in copies:
        copy.start()
    for copy in copies:
        copy.wait()
    exchange(3, out.at[at(lo_three, eighth)], out.at[at(lo_three, eighth)], second)
    exchange(4, out.at[at(lo_two, quarter)], out.at[at(lo_two, quarter)], first)
    exchange(5, out.at[at(lo_one, half)], out.at[at(lo_one, half)], swap_c)


def vmem_call(kernel, outs, name, scratch=(), flops=10**9, collective=None):
    spec = pl.BlockSpec(memory_space=pltpu.VMEM)
    if collective is None:
        params = pltpu.CompilerParams(vmem_limit_bytes=VMEM_LIMIT)
    else:
        params = pltpu.CompilerParams(vmem_limit_bytes=VMEM_LIMIT, collective_id=collective, has_side_effects=True)

    def call(*args):
        return pl.pallas_call(
            kernel,
            out_shape=[jax.ShapeDtypeStruct(s, d) for s, d in outs],
            in_specs=[spec] * len(args),
            out_specs=[spec] * len(outs),
            scratch_shapes=list(scratch),
            compiler_params=params,
            cost_estimate=pl.CostEstimate(flops=flops, bytes_accessed=4 * 10**6, transcendentals=0),
            name=name,
        )(*args)
    return call


def solution(mesh):
    parts = mesh.shape[AXIS]
    row_spec = P(AXIS, None)
    edge_spec = P(AXIS)
    rep_spec = P()
    in_specs = (row_spec, row_spec, row_spec, row_spec, edge_spec, edge_spec) + (rep_spec,) * 8 + (row_spec, row_spec)
    out_specs = (row_spec, row_spec, row_spec) + (rep_spec,) * 8

    def local_step(grid_in, mesh_static, edge_static, send_rows, edge_src, edge_dst, w_grid_in, w_mesh_in, w_edge_in, w_edge_up, w_mesh_up, w_grid_up, w_second, vectors, d_mesh_out, d_grid_out):
        lat = w_grid_up.shape[0]
        n_grid, n_feat = grid_in.shape
        n_mesh = mesh_static.shape[0]
        n_edge = edge_static.shape[0]
        n_slot = send_rows.size
        grid_t, mesh_t, edge_t = grid_in.T, mesh_static.T, edge_static.T
        send_flat = send_rows.reshape(-1)
        send_col, send_row = send_flat[:, None], send_flat[None, :]
        src_col, src_row = edge_src[:, None], edge_src[None, :]
        dst_col, dst_row = edge_dst[:, None], edge_dst[None, :]

        grid_lat, outgoing = vmem_call(grid_fwd_kernel, [((n_grid, lat), BF), ((n_slot, lat), BF)], 'grid_fwd')(
            grid_t, send_col, w_grid_in, w_second, vectors)
        incoming = lax.all_to_all(outgoing, AXIS, 0, 0, tiled=True)
        grid_out, d_lat, mesh_lat, edge_lat, recv_lat, g_a = vmem_call(
            local_kernel, [((n_grid, lat), BF), ((n_grid, lat), F32), ((n_mesh, lat), BF), ((n_edge, lat), BF), ((n_edge, lat), BF), ((2 * lat + 8, lat), F32)],
            'local', flops=4 * 10**9)(
            grid_lat, d_grid_out, mesh_t, edge_t, dst_col, w_mesh_in, w_edge_in, w_edge_up, w_grid_up, w_second, vectors)
        mesh_out, d_mesh_lat, d_edge_lat, d_pre3, d_incoming, g_b = vmem_call(
            edge_kernel,
            [((n_mesh, lat), BF), ((n_mesh, lat), F32), ((n_edge, lat), F32), ((n_edge, lat), BF), ((n_slot, lat), BF), ((7 * lat + 8, lat), F32)],
            'edge',
            scratch=[pltpu.VMEM((n_edge, lat), BF), pltpu.VMEM((n_edge, lat), BF), pltpu.VMEM((n_edge, lat), F32), pltpu.VMEM((n_edge, lat), F32),
                     pltpu.VMEM((n_edge, 128), F32), pltpu.VMEM((n_mesh, lat), BF)], flops=8 * 10**9)(
            incoming, mesh_lat, edge_lat, recv_lat, d_mesh_out, src_col, dst_col, src_row, dst_row, w_edge_up, w_mesh_up, w_second, vectors)
        d_sent = lax.all_to_all(d_incoming, AXIS, 0, 0, tiled=True)
        (g_c,) = vmem_call(embed_bwd_kernel, [((2 * lat + 24, lat), F32)], 'embed_bwd', flops=4 * 10**9)(
            mesh_t, edge_t, dst_row, d_pre3, d_mesh_lat, d_edge_lat, w_mesh_in, w_edge_in, w_edge_up, w_second, vectors)
        d_grid_t, g_d = vmem_call(grid_bwd_kernel, [((n_feat, n_grid), F32), ((lat + 176, lat), F32)], 'grid_bwd')(
            grid_t, send_row, d_sent, d_lat, w_grid_in, w_second, vectors)

        rows = g_a.shape[0] + g_b.shape[0] + g_c.shape[0] + g_d.shape[0]
        piece = -(-rows // (8 * parts)) * 8
        total = piece * parts
        (summed,) = vmem_call(
            functools.partial(sum_kernel, parts), [((total, lat), F32)], 'grad_sum',
            scratch=[pltpu.VMEM((total, lat), F32), pltpu.VMEM((16 * piece, lat), F32), pltpu.VMEM((8 * piece, lat), F32), pltpu.VMEM((4 * piece, lat), F32),
                     pltpu.VMEM((3, piece, lat), F32), pltpu.SemaphoreType.DMA((6,)), pltpu.SemaphoreType.DMA((6,)), pltpu.SemaphoreType.DMA((6,)), pltpu.SemaphoreType.DMA((6,))],
            collective=0)(g_a, g_b, g_c, g_d)
        o_b = g_a.shape[0]
        o_c = o_b + g_b.shape[0]
        o_d = o_c + g_c.shape[0]

        def cut(start, size):
            return summed[start:start + size]
        d_w_grid_up, two5, vec5 = cut(0, lat), cut(lat, lat), cut(2 * lat, 4)
        d_w_mesh_up, d_w_edge_up = cut(o_b, 2 * lat), cut(o_b + 2 * lat, 3 * lat)
        two4, two3, vec4, vec3 = cut(o_b + 5 * lat, lat), cut(o_b + 6 * lat, lat), cut(o_b + 7 * lat, 4), cut(o_b + 7 * lat + 4, 4)
        two1, two2 = cut(o_c, lat), cut(o_c + lat, lat)
        d_w_mesh_in, d_w_edge_in = cut(o_c + 2 * lat, 3), cut(o_c + 2 * lat + 8, 4)
        vec1, vec2 = cut(o_c + 2 * lat + 16, 4), cut(o_c + 2 * lat + 20, 4)
        two0, d_w_grid_in, vec0 = cut(o_d, lat), cut(o_d + lat, n_feat), cut(o_d + lat + 168, 4)
        return (mesh_out, grid_out, d_grid_t.T, d_w_grid_in, d_w_mesh_in, d_w_edge_in, d_w_edge_up, d_w_mesh_up, d_w_grid_up,
                jnp.stack([two0, two1, two2, two3, two4, two5]), jnp.stack([vec0, vec1, vec2, vec3, vec4, vec5]))

    return jax.shard_map(local_step, mesh=mesh, in_specs=in_specs, out_specs=out_specs, check_vma=False)
```

time: 464 us -> 258 us (0.56)
  Pallas kernels: 0 us -> 213 us
  other arithmetic: 115 us -> 0 us
  waiting for transfers between devices: 99.2 us -> 0.01 us
  matrix products: 73.9 us -> 0 us
  local copies, waits for them, and re-layouts: 101 us -> 29.6 us
  blocking collectives: 40.3 us -> 0 us
  between operations: 16.1 us -> 0.75 us
    pallas_call x0 -> x6, Pallas kernels: none -> 213 us  [call(): pl.pallas_call(kernel, out_shape=[jax.ShapeDtypeStruct(s, d) for s, d in...]
    psum x1 -> x0, waiting for transfers between devices: 95.3 us -> none  [local_step(): weight_grads = lax.psum(weight_grads, AXIS_NAME)]
    dot_general x43 -> x0, matrix products: 73.9 us -> none  [the longest x13 31.4 us: contract_cols(): lax.dot_general(lhs, rhs, (((1,), (1,)), ((), ())), preferred_element_typ...]
    scatter-add x4 -> x0, other arithmetic: 70.3 us -> none  [the longest x1 18.9 us: local_step(): jax.ops.segment_sum(d_pre3_wide, edge_src, num_segments=slot_rows)]
    gather x5 -> x0, local copies, waits for them, and re-layouts: 49.9 us -> none  [the longest x2 16.1 us: local_step(): d_edge_new = jnp.take(d_agg, edge_dst, axis=0)]
    psum x1 -> x0, blocking collectives: 40.3 us -> none  [local_step(): weight_grads = lax.psum(weight_grads, AXIS_NAME)]
    reduce_sum x15 -> x0, other arithmetic: 32.5 us -> none  [the longest x4 17.2 us: mlp_tail_back(): jnp.sum(d_lin, axis=0)]
    unnamed x275 -> x24, local copies, waits for them, and re-layouts: 37 us -> 11.4 us
  transfers between devices with their start and end apart: 3 -> 2, of which waited for: 2 -> 0; matrix products, arithmetic and copies ran while one was open for 15% -> 2% of each run, Pallas kernels for 0% -> 21%
where the time goes in v1:
time: 258 us; the launch traced here: 257 us
  Pallas kernels  213 us (83%)
  local copies, waits for them, and re-layouts  29.6 us (11%)
  starting transfers between devices  13.4 us (5%)
    pallas_call x6, Pallas kernels, call(): pl.pallas_call(kernel, out_shape=[jax.ShapeDtypeStruct(s, d) for s, d in...  213 us
    unnamed x24, local copies, waits for them, and re-layouts  11.4 us
    slice x6, local copies, waits for them, and re-layouts, cut(): return summed[start:start + size]  9.78 us
    all_to_all x1, starting transfers between devices, local_step(): incoming = lax.all_to_all(outgoing, AXIS, 0, 0, tiled=True)  7.36 us
    all_to_all x1, starting transfers between devices, local_step(): d_sent = lax.all_to_all(d_incoming, AXIS, 0, 0, tiled=True)  6.02 us
  transfers between devices with their start and end apart: 2, of which 0 were waited for; matrix products, arithmetic and copies ran while one was open for 2% of the time, Pallas kernels for 21%

profile of v1, /device:TPU:0, one launch (start us, length us, event | category | flops | bytes accessed | tf_op | source)
XLA Modules:
  0.0 256.5 jit_solution(13794515439447430356)
XLA Ops:
  0.6 2.7 %broadcast_in_dim_reshape.8.send_col = s32[2048,1]{1,0:T(8,128)} reshape(s32[32,64]{1,0:T(8,128)} %param.19) | data formatting | bytes 16384 | tf_op jit(solution)/shard_map/broadcast_in_dim;reshape | solution.py:350
  3.3 10.8 %grid_fwd.1 = (bf16[2048,256]{1,0:T(8,128)(2,1)}, bf16[2048,256]{1,0:T(8,128)(2,1)}) custom-call(bf16[164,2048]{1,0:T(8,128)(2,1)} %bitcast.40, s32[2048,1]{1,0:T(8,128)} %broadcast_in_dim_reshape.8.send_col, bf16[164,256]{1,0:T(8,128)(2,1)} %w_grid_in.3, bf16[6,256,256]{2,1,0:T(8,128)(2,1)} %w_two.9, f32[6,4,256]{2,1,0:T(4,128)} %vec.9), custom_call_target="tpu_custom_call" | custom-call | flops 1000000000 | bytes 4000000 | tf_op jit(solution)/shard_map/grid_fwd/pallas_call | solution.py:321
  14.2 0.0 copy-start.5
  14.2 0.0 copy-start.4
  14.2 7.4 %all-to-all-start = ((bf16[32,64,256]{2,1,0:T(8,128)(2,1)}), bf16[32,64,256]{2,1,0:T(8,128)(2,1)S(1)}, u32[]{:S(2)}, u32[]{:S(2)}) async-start(bf16[32,64,256]{2,1,0:T(8,128)(2,1)} %bitcast.39), calls=%async_computation | async-start | bytes 2097152 | tf_op jit(solution)/shard_map/all_to_all | solution.py:356
  21.5 0.0 copy-done.5
  21.5 1.7 copy.28.dst_col
  23.2 0.0 copy-done.4
  23.2 1.7 copy.29.src_col
  24.9 24.6 %local.1 = (bf16[2048,256]{1,0:T(8,128)(2,1)}, f32[2048,256]{1,0:T(8,128)}, bf16[2048,256]{1,0:T(8,128)(2,1)}, bf16[3072,256]{1,0:T(8,128)(2,1)}, bf16[3072,256]{1,0:T(8,128)(2,1)}, /*index=5*/f32[520,256]{1,0:T(8,128)}) custom-call(bf16[2048,256]{1,0:T(8,128)(2,1)} %get-tuple-element.28.grid_lat, bf16[2048,256]{1,0:T(8,128)(2,1)} %d_grid.1, ...), custom_call_target="tpu_custom_call" | custom-call | flops 4000000000 | bytes 4000000 | tf_op jit(solution)/shard_map/local/pallas_call | solution.py:321
  49.5 0.0 all-to-all-done
  49.6 0.0 copy-start.1
  49.6 1.0 copy-done.1
  50.5 62.9 %edge.1 = (bf16[2048,256]{1,0:T(8,128)(2,1)}, f32[2048,256]{1,0:T(8,128)}, f32[3072,256]{1,0:T(8,128)}, bf16[3072,256]{1,0:T(8,128)(2,1)}, bf16[2048,256]{1,0:T(8,128)(2,1)}, /*index=5*/f32[1800,256]{1,0:T(8,128)}) custom-call(bf16[2048,256]{1,0:T(8,128)(2,1)} %bitcast.37, bf16[2048,256]{1,0:T(8,128)(2,1)} %get-tuple-element.29.mesh_lat, ...), custom_call_target="tpu_custom_call" | custom-call | flops 8000000000 | bytes 4000000 | tf_op jit(solution)/shard_map/edge/pallas_call | solution.py:321
  113.4 0.0 copy-start.2
  113.4 6.0 %all-to-all-start.1 = ((bf16[32,64,256]{2,1,0:T(8,128)(2,1)}), bf16[32,64,256]{2,1,0:T(8,128)(2,1)S(1)}, u32[]{:S(2)}, u32[]{:S(2)}) async-start(bf16[32,64,256]{2,1,0:T(8,128)(2,1)} %bitcast.38), calls=%async_computation.1 | async-start | bytes 2097152 | tf_op jit(solution)/shard_map/all_to_all | solution.py:368
  119.5 0.0 copy-done.2
  119.5 0.7 broadcast_in_dim_reshape.7.send_row
  120.1 28.6 %embed_bwd.1.g_c = f32[536,256]{1,0:T(8,128)} custom-call(bf16[3,2048]{1,0:T(4,128)(2,1)} %bitcast.51, bf16[4,3072]{1,0:T(4,128)(2,1)} %bitcast.49, s32[1,3072]{1,0:T(1,128)} %bitcast.45, bf16[3072,256]{1,0:T(8,128)(2,1)} %get-tuple-element.39.d_pre3, f32[2048,256]{1,0:T(8,128)} %get-tuple-element.40.d_mesh_lat, f32[3072,256]{1,0:T(8,128)} %get-tuple-element.41.d_edge_lat, ...), custom_call_target="tpu_custom_call" | custom-call | flops 4000000000 | bytes 4000000 | tf_op jit(solution)/shard_map/embed_bwd/pallas_call | solution.py:321
  148.7 0.0 all-to-all-done.1
  148.7 0.0 copy-start
  148.7 1.0 copy-done
  149.7 13.4 %grid_bwd.1 = (f32[164,2048]{1,0:T(8,128)}, f32[432,256]{1,0:T(8,128)}) custom-call(bf16[164,2048]{1,0:T(8,128)(2,1)} %bitcast.41, s32[1,2048]{1,0:T(1,128)} %broadcast_in_dim_reshape.7.send_row, bf16[2048,256]{1,0:T(8,128)(2,1)} %bitcast.36, f32[2048,256]{1,0:T(8,128)} %get-tuple-element.35.d_lat, bf16[164,256]{1,0:T(8,128)(2,1)} %w_grid_in.3, ...), custom_call_target="tpu_custom_call" | custom-call | flops 1000000000 | bytes 4000000 | tf_op jit(solution)/shard_map/grid_bwd/pallas_call | solution.py:321
  163.1 72.4 %grad_sum.1 = f32[3328,256]{1,0:T(8,128)} custom-call(f32[520,256]{1,0:T(8,128)} %get-tuple-element.37.g_a, f32[1800,256]{1,0:T(8,128)} %get-tuple-element.38.g_b, f32[536,256]{1,0:T(8,128)} %embed_bwd.1.g_c, f32[432,256]{1,0:T(8,128)} %get-tuple-element.42.g_d), custom_call_target="tpu_custom_call" | custom-call | flops 1000000000 | bytes 4000000 | tf_op jit(solution)/shard_map/grad_sum/pallas_call | solution.py:321
  235.5 0.7 constant_dynamic-update-slice_fusion.5
  236.2 1.0 bitcast_dynamic-update-slice_fusion.5
  237.2 2.1 slice.57
  239.3 1.9 slice.58
  241.1 1.7 slice.59
  242.8 1.6 slice.54
  244.4 1.3 slice.55
  245.7 1.3 slice.56
  247.0 0.7 constant_dynamic-update-slice_fusion.4
  247.7 0.7 constant_dynamic-update-slice_fusion.3
  248.4 0.7 constant_dynamic-update-slice_fusion.2
  249.1 0.7 constant_dynamic-update-slice_fusion.1
  249.8 0.7 constant_dynamic-update-slice_fusion
  250.5 0.0 copy-start.6
  250.5 1.0 bitcast_dynamic-update-slice_fusion.4
  251.5 1.0 bitcast_dynamic-update-slice_fusion.3
  252.5 1.0 bitcast_dynamic-update-slice_fusion.2
  253.4 1.0 bitcast_dynamic-update-slice_fusion.1
  254.4 1.0 bitcast_dynamic-update-slice_fusion
  255.4 0.0 copy-start.3
  255.4 0.0 copy-done.6
  255.4 1.1 copy-done.3
Async XLA Ops:
  14.2 7.4 %copy-start.5 = (s32[3072]{0:T(1024)S(1)}, s32[3072]{0:T(1024)}, u32[]{:S(2)}) copy-start(s32[3072]{0:T(1024)} %param.21) | copy-start | bytes 36868
  14.2 9.0 %copy-start.4 = (s32[3072]{0:T(1024)S(1)}, s32[3072]{0:T(1024)}, u32[]{:S(2)}) copy-start(s32[3072]{0:T(1024)} %param.20) | copy-start | bytes 36868
  14.2 35.4 %all-to-all-start = ((bf16[32,64,256]{2,1,0:T(8,128)(2,1)}), bf16[32,64,256]{2,1,0:T(8,128)(2,1)S(1)}, u32[]{:S(2)}, u32[]{:S(2)}) async-start(bf16[32,64,256]{2,1,0:T(8,128)(2,1)} %bitcast.39), calls=%async_computation | async-start | bytes 2097152 | tf_op jit(solution)/shard_map/all_to_all | solution.py:356
  49.6 1.0 copy-start.1
  113.4 6.0 %copy-start.2 = (s32[32,64]{1,0:T(8,128)S(1)}, s32[32,64]{1,0:T(8,128)}, u32[]{:S(2)}) copy-start(s32[32,64]{1,0:T(8,128)} %param.19) | copy-start | bytes 24580
  113.4 35.3 %all-to-all-start.1 = ((bf16[32,64,256]{2,1,0:T(8,128)(2,1)}), bf16[32,64,256]{2,1,0:T(8,128)(2,1)S(1)}, u32[]{:S(2)}, u32[]{:S(2)}) async-start(bf16[32,64,256]{2,1,0:T(8,128)(2,1)} %bitcast.38), calls=%async_computation.1 | async-start | bytes 2097152 | tf_op jit(solution)/shard_map/all_to_all | solution.py:368
  148.7 1.0 copy-start
  250.5 4.9 %copy-start.6 = (f32[6,4,256]{2,1,0:T(4,128)}, f32[6,4,256]{2,1,0:T(4,128)S(1)}, u32[]{:S(2)}) copy-start(f32[6,4,256]{2,1,0:T(4,128)S(1)} %constant_dynamic-update-slice_fusion) | copy-start | bytes 73732
  255.4 1.1 copy-start.3

commit v2 on v1

v2 whole, which is shorter than its diff:
```python
import functools

import jax
import jax.numpy as jnp
from jax import lax
from jax.experimental import pallas as pl
from jax.experimental.pallas import tpu as pltpu
from jax.sharding import PartitionSpec as P

LN_EPS = 1e-5
AXIS = 'gp'
BF = jnp.bfloat16
F32 = jnp.float32
MESH = pl.DeviceIdType.MESH
TILE = 256
VMEM_LIMIT = 60 * 1024 * 1024


def nn(lhs, rhs):
    return jnp.dot(lhs, rhs, preferred_element_type=F32)


def tn(lhs, rhs):
    return lax.dot_general(lhs, rhs, (((0,), (0,)), ((), ())), preferred_element_type=F32)


def nt(lhs, rhs):
    return lax.dot_general(lhs, rhs, (((1,), (1,)), ((), ())), preferred_element_type=F32)


def mlp_fwd(pre_act, w_two, vec):
    act = pre_act + vec[0:1]
    sig = 0.5 * jnp.tanh(0.5 * act) + 0.5
    hidden = (act * sig).astype(BF)
    lin = nn(hidden, w_two) + vec[1:2]
    cen = lin - jnp.mean(lin, axis=-1, keepdims=True)
    inv = lax.rsqrt(jnp.mean(cen * cen, axis=-1, keepdims=True) + LN_EPS)
    normed = cen * inv
    return (act, sig, hidden, normed, inv), normed * vec[2:3] + vec[3:4]


def mlp_bwd(saved, w_two, vec, d_out):
    act, sig, hidden, normed, inv = saved
    d_n = d_out * vec[2:3]
    m_one = jnp.mean(d_n, axis=-1, keepdims=True)
    m_two = jnp.mean(d_n * normed, axis=-1, keepdims=True)
    d_lin = inv * (d_n - m_one - normed * m_two)
    d_lin_bf = d_lin.astype(BF)
    d_two = tn(hidden, d_lin_bf)
    d_hid = nt(d_lin_bf, w_two)
    d_pre = d_hid * (sig * (1.0 + act * (1.0 - sig)))
    d_vec = [jnp.sum(d_pre, axis=0, keepdims=True), jnp.sum(d_lin, axis=0, keepdims=True),
             jnp.sum(d_out * normed, axis=0, keepdims=True), jnp.sum(d_out, axis=0, keepdims=True)]
    return d_pre.astype(BF), d_two, d_vec


def add_vec(ref, base, d_vec):
    for j in range(4):
        ref[base + j:base + j + 1, :] += d_vec[j]


def rows_at(i, size=TILE):
    return pl.ds(pl.multiple_of(i * size, size), size)


def hot_cols(col_idx, width):
    ids = lax.broadcasted_iota(jnp.int32, (col_idx.shape[0], width), 1)
    return jnp.where(ids == col_idx, 1.0, 0.0).astype(BF)


def hot_rows(row_idx, base, height):
    ids = lax.broadcasted_iota(jnp.int32, (height, row_idx.shape[1]), 0) + base
    return jnp.where(ids == row_idx, 1.0, 0.0).astype(BF)


def col_of(idx_ref, i):
    cols = []
    for j in range(TILE // 128):
        row = idx_ref[pl.ds(i * (TILE // 128) + j, 1), :]
        cols.append(jnp.transpose(jnp.broadcast_to(row, (8, 128)))[:, 0:1])
    return jnp.concatenate(cols, axis=0)


def fill_row(idx_ref, row_ref):
    for j in range(idx_ref.shape[0]):
        row_ref[0:1, j * 128:(j + 1) * 128] = idx_ref[j:j + 1, :]


def loop(n, body, events=()):
    def step(i, carry):
        body(i)
        for when, fn in events:
            pl.when(i == when)(fn)
        return carry
    lax.fori_loop(0, n, step, 0)


class Reducer:
    def __init__(self, group, base, rows, place, refs):
        self.own, self.out, r_one, r_two, r_three, r_four, self.send_sem, self.recv_sem = refs
        self.group, self.place = group, place
        self.piece = rows // 32
        self.half, self.quarter, self.eighth = rows // 2, rows // 4, rows // 8
        self.r_one = r_one.at[pl.ds(base // 2, rows // 2)]
        self.r_two = r_two.at[pl.ds(base // 4, rows // 4)]
        self.r_three = r_three.at[pl.ds(base // 8, rows // 8)]
        self.r_four = [r_four.at[k, pl.ds(base // 32, rows // 32)] for k in range(3)]
        self.lo_one = base + place['core'] * self.half
        self.lo_two = self.lo_one + place['bit_one'] * self.quarter
        self.lo_three = self.lo_two + place['bit_two'] * self.eighth
        self.lo_four = self.lo_three + place['z'] * self.piece

    def at(self, start, size):
        return pl.ds(pl.multiple_of(start, 8), size)

    def copies(self, k):
        place, own, out = self.place, self.own, self.out

        def make(slot, src, dst, peer):
            return pltpu.make_async_remote_copy(src_ref=src, dst_ref=dst, send_sem=self.send_sem.at[self.group, slot],
                                                recv_sem=self.recv_sem.at[self.group, slot], device_id=(peer,), device_id_type=MESH)
        if k == 0:
            lo = self.lo_one + (1 - 2 * place['core']) * self.half
            return [make(0, own.at[self.at(lo, self.half)], self.r_one, place['swap_c'])]
        if k == 1:
            lo = self.lo_two + (1 - 2 * place['bit_one']) * self.quarter
            return [make(1, own.at[self.at(lo, self.quarter)], self.r_two, place['first'])]
        if k == 2:
            lo = self.lo_three + (1 - 2 * place['bit_two']) * self.eighth
            return [make(2, own.at[self.at(lo, self.eighth)], self.r_three, place['second'])]
        if k == 3:
            return [make(3 + j, own.at[self.at(self.lo_three + place['z_to'][j] * self.piece, self.piece)], self.r_four[j], place['z_dev'][j]) for j in range(3)]
        if k == 4:
            sl = self.at(self.lo_four, self.piece)
            return [make(6 + j, out.at[sl], out.at[sl], place['z_dev'][j]) for j in range(3)]
        sl = self.at(*((self.lo_three, self.eighth), (self.lo_two, self.quarter), (self.lo_one, self.half))[k - 5])
        return [make(4 + k, out.at[sl], out.at[sl], place[('second', 'first', 'swap_c')[k - 5]])]

    def start(self, k):
        for copy in self.copies(k):
            copy.start()

    def finish(self, k):
        for copy in self.copies(k):
            copy.wait()
        if k == 0:
            sl = self.at(self.lo_one, self.half)
            self.own[sl, :] += self.r_one[...]
        if k == 1:
            sl = self.at(self.lo_two, self.quarter)
            self.own[sl, :] += self.r_two[...]
        if k == 2:
            sl = self.at(self.lo_three, self.eighth)
            self.own[sl, :] += self.r_three[...]
        if k == 3:
            sl = self.at(self.lo_four, self.piece)
            self.out[sl, :] = self.own[sl, :] + (self.r_four[0][...] + self.r_four[1][...] + self.r_four[2][...])

    def step(self, k):
        def fn():
            if k > 0:
                self.finish(k - 1)
            if k < 8:
                self.start(k)
        return fn


def step_kernel(parts, grid_t, mesh_t, edge_t, send_idx, src_idx, dst_idx, w_grid_in, w_mesh_in, w_edge_in, w_two, vec,
                w_edge_up_h, w_mesh_up_h, w_grid_up_h, d_mesh_h, d_grid_h,
                mesh_out_h, grid_out_h, d_grid_t_h, d_wgi, d_wmi, d_wei, d_weu, d_wmu, d_wgu, d_two, d_vec_out,
                w_edge_up, w_mesh_up, w_grid_up, d_mesh, d_grid, mesh_out, grid_out, d_grid_t,
                grid_lat, outgoing, incoming, d_lat, mesh_lat, edge_lat, recv_lat, send_lat, edge_new, act_s, nrm_s, inv_s,
                d_pre4, d_mesh_lat, d_edge_lat, d_pre3, d_incoming, d_sent, send_row, src_row, dst_row,
                own, out, r_one, r_two, r_three, r_four,
                in_sem, out_sem, go_send, go_recv, back_send, back_recv, red_send, red_recv):
    lat = w_two.shape[1]
    n_feat, n_grid = grid_t.shape
    n_mesh, n_edge, n_slot = mesh_lat.shape[0], edge_lat.shape[0], outgoing.shape[0]
    cap = n_slot // parts
    per_tile = TILE // cap
    n_feat_pad = -(-n_feat // 8) * 8
    me = lax.axis_index(AXIS)
    core = lax.rem(me, 2)
    x_at = lax.rem(me // 2, 2)
    y_at = lax.rem(me // 4, 2)
    z_at = me // 8
    plane = me - 8 * z_at
    swap_x = me + 2 * (1 - 2 * x_at)
    swap_y = me + 4 * (1 - 2 * y_at)
    z_to = [lax.rem(z_at + k, 4) for k in range(1, 4)]
    place = dict(core=core, z=z_at, swap_c=me + 1 - 2 * core,
                 first=(1 - core) * swap_x + core * swap_y, second=(1 - core) * swap_y + core * swap_x,
                 bit_one=(1 - core) * x_at + core * y_at, bit_two=(1 - core) * y_at + core * x_at,
                 z_to=z_to, z_dev=[plane + 8 * z for z in z_to])

    barrier = pltpu.get_barrier_semaphore()

    def knock(k, carry):
        pl.semaphore_signal(barrier, inc=1, device_id=(lax.rem(me + k, parts),), device_id_type=MESH)
        return carry
    lax.fori_loop(1, parts, knock, 0)

    loads = [pltpu.make_async_copy(a, b, in_sem.at[k]) for k, (a, b) in enumerate(
        [(d_grid_h, d_grid), (w_grid_up_h, w_grid_up), (w_edge_up_h, w_edge_up), (w_mesh_up_h, w_mesh_up), (d_mesh_h, d_mesh)])]
    for copy in loads:
        copy.start()

    r_wgu, r_two5, r_wmu, r_two4 = 0, lat, 2 * lat, 4 * lat
    r_weu, r_two3 = 5 * lat, 8 * lat
    r_two1, r_two2 = 9 * lat, 10 * lat
    r_two0, r_wgi = 11 * lat, 12 * lat
    r_wmi = r_wgi + n_feat_pad
    r_wei = r_wmi + 8
    r_vec = r_wei + 8
    refs = (own, out, r_one, r_two, r_three, r_four, red_send, red_recv)
    bounds = [0, 5 * lat, 9 * lat, 11 * lat, own.shape[0]]
    red = [Reducer(g, bounds[g], bounds[g + 1] - bounds[g], place, refs) for g in range(4)]

    own[...] = jnp.zeros_like(own)
    fill_row(send_idx, send_row)
    fill_row(src_idx, src_row)
    fill_row(dst_idx, dst_row)

    def embed(i):
        sl = rows_at(i)
        _, emb = mlp_fwd(tn(grid_t[:, sl], w_grid_in[...]), w_two[0], vec[0])
        grid_lat[sl, :] = emb.astype(BF)
    loop(n_grid // TILE, embed)

    pl.semaphore_wait(barrier, parts - 1)

    def part_copy(src, dst, sends, recvs, to, frm):
        return pltpu.make_async_remote_copy(
            src_ref=src.at[pl.ds(pl.multiple_of(to * cap, 8), cap)], dst_ref=dst.at[pl.ds(pl.multiple_of(frm * cap, 8), cap)],
            send_sem=sends.at[to], recv_sem=recvs.at[frm], device_id=(to,), device_id_type=MESH)

    def send_tile(src, dst, sends, recvs, tile):
        for j in range(per_tile):
            to = tile * per_tile + j

            @pl.when(to != me)
            def _():
                part_copy(src, dst, sends, recvs, to, me).start()

            @pl.when(to == me)
            def _():
                own_sl = pl.ds(pl.multiple_of(me * cap, 8), cap)
                dst[own_sl, :] = src[own_sl, :]

    def wait_all(src, dst, sends, recvs):
        def one(k, carry):
            other = lax.rem(me + k, parts)
            part_copy(src, dst, sends, recvs, other, me).wait_send()
            part_copy(src, dst, sends, recvs, me, other).wait_recv()
            return carry
        lax.fori_loop(1, parts, one, 0)

    slot_tiles = n_slot // TILE
    my_tile = me // per_tile

    def turn(i):
        return lax.rem(my_tile + slot_tiles // 2 + i, slot_tiles)

    def pick(i):
        tile = turn(i)
        sl = rows_at(tile)
        outgoing[sl, :] = nn(hot_cols(col_of(send_idx, tile), n_grid), grid_lat[...]).astype(BF)
        send_tile(outgoing, incoming, go_send, go_recv, tile)
    loop(slot_tiles, pick)

    loads[0].wait()
    loads[1].wait()

    def cells(i):
        sl = rows_at(i)
        here = grid_lat[sl, :]
        saved, upd = mlp_fwd(nn(here, w_grid_up[...]), w_two[5], vec[5])
        grid_out[sl, :] = (here.astype(F32) + upd).astype(BF)
        d_top = d_grid[sl, :].astype(F32)
        d_pre, d_two5, d_vec = mlp_bwd(saved, w_two[5], vec[5], d_top)
        own[r_wgu:r_wgu + lat, :] += tn(here, d_pre)
        own[r_two5:r_two5 + lat, :] += d_two5
        add_vec(own, r_vec + 20, d_vec)
        d_lat[sl, :] = d_top + nt(d_pre, w_grid_up[...])
    loop(n_grid // TILE, cells)
    stores = [pltpu.make_async_copy(a, b, out_sem.at[k]) for k, (a, b) in enumerate([(grid_out, grid_out_h), (mesh_out, mesh_out_h), (d_grid_t, d_grid_t_h)])]
    stores[0].start()

    def nodes_in(i):
        sl = rows_at(i)
        _, emb = mlp_fwd(tn(mesh_t[:, sl], w_mesh_in[...]), w_two[1], vec[1])
        mesh_lat[sl, :] = emb.astype(BF)
    loop(n_mesh // TILE, nodes_in)

    def edges_in(i):
        sl = rows_at(i)
        _, emb = mlp_fwd(tn(edge_t[:, sl], w_edge_in[...]), w_two[2], vec[2])
        edge_lat[sl, :] = emb.astype(BF)
        recv_lat[sl, :] = nn(hot_cols(col_of(dst_idx, i), n_mesh), mesh_lat[...]).astype(BF)
    loop(n_edge // TILE, edges_in)

    loads[2].wait()
    loads[3].wait()
    loads[4].wait()
    wait_all(outgoing, incoming, go_send, go_recv)

    def edges_fwd(i):
        sl = rows_at(i)
        sent = nn(hot_cols(col_of(src_idx, i), n_slot), incoming[...]).astype(BF)
        send_lat[sl, :] = sent
        here = edge_lat[sl, :]
        pre = nn(here, w_edge_up[0:lat, :]) + nn(sent, w_edge_up[lat:2 * lat, :]) + nn(recv_lat[sl, :], w_edge_up[2 * lat:3 * lat, :])
        (act, _, _, normed, inv), upd = mlp_fwd(pre, w_two[3], vec[3])
        act_s[sl, :] = act
        nrm_s[sl, :] = normed
        inv_s[sl, :] = jnp.broadcast_to(inv, (TILE, 128))
        edge_new[sl, :] = (here.astype(F32) + upd).astype(BF)
    loop(n_edge // TILE, edges_fwd)

    def nodes(i):
        sl = rows_at(i)
        agg = nn(hot_rows(dst_row[...], i * TILE, TILE), edge_new[...]).astype(BF)
        here = mesh_lat[sl, :]
        saved, upd = mlp_fwd(nn(here, w_mesh_up[0:lat, :]) + nn(agg, w_mesh_up[lat:2 * lat, :]), w_two[4], vec[4])
        mesh_out[sl, :] = (here.astype(F32) + upd).astype(BF)
        d_top = d_mesh[sl, :].astype(F32)
        d_pre, d_two4, d_vec = mlp_bwd(saved, w_two[4], vec[4], d_top)
        d_pre4[sl, :] = d_pre
        own[r_wmu:r_wmu + lat, :] += tn(here, d_pre)
        own[r_wmu + lat:r_wmu + 2 * lat, :] += tn(agg, d_pre)
        own[r_two4:r_two4 + lat, :] += d_two4
        add_vec(own, r_vec + 16, d_vec)
        d_mesh_lat[sl, :] = d_top + nt(d_pre, w_mesh_up[0:lat, :])
    loop(n_mesh // TILE, nodes)
    stores[1].start()

    def edges_bwd(i):
        sl = rows_at(i)
        picked = nn(hot_cols(col_of(dst_idx, i), n_mesh), d_pre4[...]).astype(BF)
        d_new = nt(picked, w_mesh_up[lat:2 * lat, :])
        act = act_s[sl, :]
        sig = 0.5 * jnp.tanh(0.5 * act) + 0.5
        hidden = (act * sig).astype(BF)
        d_pre, d_two3, d_vec = mlp_bwd((act, sig, hidden, nrm_s[sl, :], inv_s[sl, 0:1]), w_two[3], vec[3], d_new)
        d_pre3[sl, :] = d_pre
        own[r_two3:r_two3 + lat, :] += d_two3
        add_vec(own, r_vec + 12, d_vec)
        own[r_weu:r_weu + lat, :] += tn(edge_lat[sl, :], d_pre)
        own[r_weu + lat:r_weu + 2 * lat, :] += tn(send_lat[sl, :], d_pre)
        own[r_weu + 2 * lat:r_weu + 3 * lat, :] += tn(recv_lat[sl, :], d_pre)
        d_edge_lat[sl, :] = d_new + nt(d_pre, w_edge_up[0:lat, :])
    n_et, n_nt, n_gt = n_edge // TILE, n_mesh // TILE, n_grid // TILE
    red[0].start(0)
    loop(n_et, edges_bwd, [(n_et * 2 // 12, red[0].step(1)), (n_et * 7 // 12, red[0].step(2)), (n_et - 1, red[0].step(3))])

    red[1].start(0)

    def slots(i):
        tile = turn(i)
        sl = rows_at(tile)
        d_slot = nn(hot_rows(src_row[...], tile * TILE, TILE), d_pre3[...]).astype(BF)
        d_incoming[sl, :] = nt(d_slot, w_edge_up[lat:2 * lat, :]).astype(BF)
        send_tile(d_incoming, d_sent, back_send, back_recv, tile)
    loop(slot_tiles, slots, [(slot_tiles - 1, red[1].step(1))])

    def nodes_bwd(i):
        sl = rows_at(i)
        d_node = nn(hot_rows(dst_row[...], i * TILE, TILE), d_pre3[...]).astype(BF)
        d_top = d_mesh_lat[sl, :] + nt(d_node, w_edge_up[2 * lat:3 * lat, :])
        feat = mesh_t[:, sl]
        saved, _ = mlp_fwd(tn(feat, w_mesh_in[...]), w_two[1], vec[1])
        d_pre, d_two1, d_vec = mlp_bwd(saved, w_two[1], vec[1], d_top)
        own[r_two1:r_two1 + lat, :] += d_two1
        own[r_wmi:r_wmi + 3, :] += nn(feat, d_pre)
        add_vec(own, r_vec + 4, d_vec)
    loop(n_nt, nodes_bwd, [(n_nt * 2 // 8, red[0].step(4)), (n_nt - 1, red[1].step(2))])

    def edges_in_bwd(i):
        sl = rows_at(i)
        feat = edge_t[:, sl]
        saved, _ = mlp_fwd(tn(feat, w_edge_in[...]), w_two[2], vec[2])
        d_pre, d_two2, d_vec = mlp_bwd(saved, w_two[2], vec[2], d_edge_lat[sl, :])
        own[r_two2:r_two2 + lat, :] += d_two2
        own[r_wei:r_wei + 4, :] += nn(feat, d_pre)
        add_vec(own, r_vec + 8, d_vec)
    loop(n_et, edges_in_bwd, [(n_et * 2 // 12, red[0].step(5)), (n_et * 5 // 12, red[1].step(3)), (n_et * 7 // 12, red[0].step(6)), (n_et - 1, red[0].step(7))])

    red[2].start(0)
    wait_all(d_incoming, d_sent, back_send, back_recv)
    red[1].step(4)()

    def grid_bwd(i):
        sl = rows_at(i)
        d_top = d_lat[sl, :] + nn(hot_rows(send_row[...], i * TILE, TILE), d_sent[...])
        feat = grid_t[:, sl]
        saved, _ = mlp_fwd(tn(feat, w_grid_in[...]), w_two[0], vec[0])
        d_pre, d_two0, d_vec = mlp_bwd(saved, w_two[0], vec[0], d_top)
        own[r_two0:r_two0 + lat, :] += d_two0
        own[r_wgi:r_wgi + n_feat, :] += nn(feat, d_pre)
        add_vec(own, r_vec, d_vec)
        d_grid_t[:, sl] = nt(w_grid_in[...], d_pre)
    loop(n_gt, grid_bwd, [(0, red[2].step(1)), (n_gt * 2 // 8, red[0].step(8)), (n_gt * 3 // 8, red[1].step(5)), (n_gt * 4 // 8, red[2].step(2)), (n_gt * 5 // 8, red[1].step(6)), (n_gt - 1, red[2].step(3))])
    stores[2].start()

    red[3].start(0)
    red[1].step(7)()
    red[3].step(1)()
    red[2].step(4)()
    red[1].step(8)()
    red[3].step(2)()
    red[2].step(5)()
    red[3].step(3)()
    red[2].step(6)()
    red[3].step(4)()
    red[2].step(7)()
    red[2].step(8)()
    puts = [(r_weu, 3 * lat, d_weu), (r_wmu, 2 * lat, d_wmu), (r_wgu, lat, d_wgu), (r_two1, lat, d_two.at[1]),
            (r_two2, lat, d_two.at[2]), (r_two3, lat, d_two.at[3]), (r_two4, lat, d_two.at[4]), (r_two5, lat, d_two.at[5])]
    moves = [pltpu.make_async_copy(out.at[pl.ds(a, n)], ref, out_sem.at[3 + k]) for k, (a, n, ref) in enumerate(puts)]
    for move in moves:
        move.start()
    for k in range(5, 9):
        red[3].step(k)()
    last = pltpu.make_async_copy(out.at[pl.ds(r_two0, lat)], d_two.at[0], out_sem.at[11])
    last.start()
    d_wgi[...] = out[r_wgi:r_wgi + n_feat, :]
    d_wmi[...] = out[r_wmi:r_wmi + 3, :]
    d_wei[...] = out[r_wei:r_wei + 4, :]
    for k in range(6):
        d_vec_out[k] = out[r_vec + 4 * k:r_vec + 4 * k + 4, :]
    for copy in stores + moves + [last]:
        copy.wait()


def solution(mesh):
    parts = mesh.shape[AXIS]
    row_spec = P(AXIS, None)
    edge_spec = P(AXIS)
    rep_spec = P()
    in_specs = (row_spec, row_spec, row_spec, row_spec, edge_spec, edge_spec) + (rep_spec,) * 8 + (row_spec, row_spec)
    out_specs = (row_spec, row_spec, row_spec) + (rep_spec,) * 8

    def local_step(grid_in, mesh_static, edge_static, send_rows, edge_src, edge_dst, w_grid_in, w_mesh_in, w_edge_in, w_edge_up, w_mesh_up, w_grid_up, w_second, vectors, d_mesh_out, d_grid_out):
        lat = w_grid_up.shape[0]
        n_grid, n_feat = grid_in.shape
        n_mesh = mesh_static.shape[0]
        n_edge = edge_static.shape[0]
        n_slot = send_rows.size
        small = -(-n_feat // 8) * 8 + 8 + 8 + 24
        total = 11 * lat + -(-(lat + small) // 256) * 256
        near = pl.BlockSpec(memory_space=pltpu.VMEM)
        far = pl.BlockSpec(memory_space=pl.ANY)

        def sds(shape, dtype):
            return jax.ShapeDtypeStruct(shape, dtype)
        outs = [sds((n_mesh, lat), BF), sds((n_grid, lat), BF), sds((n_feat, n_grid), F32), sds(w_grid_in.shape, F32), sds(w_mesh_in.shape, F32), sds(w_edge_in.shape, F32),
                sds(w_edge_up.shape, F32), sds(w_mesh_up.shape, F32), sds(w_grid_up.shape, F32), sds(w_second.shape, F32), sds(vectors.shape, F32)]
        out_specs = [far, far, far, near, near, near, far, far, far, far, near]
        V = pltpu.VMEM
        D = pltpu.SemaphoreType.DMA
        scratch = [V(w_edge_up.shape, BF), V(w_mesh_up.shape, BF), V(w_grid_up.shape, BF), V((n_mesh, lat), BF), V((n_grid, lat), BF),
                   V((n_mesh, lat), BF), V((n_grid, lat), BF), V((n_feat, n_grid), F32),
                   V((n_grid, lat), BF), V((n_slot, lat), BF), V((n_slot, lat), BF), V((n_grid, lat), F32), V((n_mesh, lat), BF),
                   V((n_edge, lat), BF), V((n_edge, lat), BF), V((n_edge, lat), BF), V((n_edge, lat), BF), V((n_edge, lat), F32), V((n_edge, lat), F32), V((n_edge, 128), F32),
                   V((n_mesh, lat), BF), V((n_mesh, lat), F32), V((n_edge, lat), F32), V((n_edge, lat), BF), V((n_slot, lat), BF), V((n_slot, lat), BF),
                   V((1, n_slot), jnp.int32), V((1, n_edge), jnp.int32), V((1, n_edge), jnp.int32),
                   V((total, lat), F32), V((total, lat), F32), V((total // 2, lat), F32), V((total // 4, lat), F32), V((total // 8, lat), F32), V((3, total // 32, lat), F32),
                   D((5,)), D((12,)), D((parts,)), D((parts,)), D((parts,)), D((parts,)), D((4, 12)), D((4, 12))]
        res = pl.pallas_call(
            functools.partial(step_kernel, parts),
            out_shape=outs,
            in_specs=[near] * 11 + [far] * 5,
            out_specs=out_specs,
            scratch_shapes=scratch,
            compiler_params=pltpu.CompilerParams(vmem_limit_bytes=VMEM_LIMIT, collective_id=0, has_side_effects=True),
            name='step',
        )(grid_in.T, mesh_static.T, edge_static.T, send_rows.reshape(-1, 128), edge_src.reshape(-1, 128), edge_dst.reshape(-1, 128),
          w_grid_in, w_mesh_in, w_edge_in, w_second, vectors, w_edge_up, w_mesh_up, w_grid_up, d_mesh_out, d_grid_out)
        return (res[0], res[1], res[2].T) + tuple(res[3:])

    return jax.shard_map(local_step, mesh=mesh, in_specs=in_specs, out_specs=out_specs, check_vma=False)
```

time: 258 us -> 186 us (0.72)
  Pallas kernels: 213 us -> 173 us
  local copies, waits for them, and re-layouts: 29.6 us -> 11.9 us
  starting transfers between devices: 13.4 us -> 0 us
    pallas_call x6 -> x1, Pallas kernels: 213 us -> 173 us  [local_step(): pl.pallas_call(functools.partial(step_kernel, parts), out_shape=outs, in_...]
    all_to_all x2 -> x0, starting transfers between devices: 13.4 us -> none  [the longest x1 7.36 us: local_step(): incoming = lax.all_to_all(outgoing, AXIS, 0, 0, tiled=True)]
    slice x6 -> x0, local copies, waits for them, and re-layouts: 9.78 us -> none  [cut(): return summed[start:start + size]]
    another operation x4 -> x0, local copies, waits for them, and re-layouts: 5.05 us -> none  [the longest x2 3.38 us: local_step(): send_col, send_row = (send_flat[:, None], send_flat[None, :])]
    broadcast_in_dim x2 -> x0, local copies, waits for them, and re-layouts: 3.37 us -> none  [the longest x1 1.71 us: local_step(): src_col, src_row = (edge_src[:, None], edge_src[None, :])]
    unnamed x24 -> x31, local copies, waits for them, and re-layouts: 11.4 us -> 10.5 us
  transfers between devices with their start and end apart: 2 -> 0, of which waited for: 0 -> 0; matrix products, arithmetic and copies ran while one was open for 2% -> 0% of each run, Pallas kernels for 21% -> 0%
where the time goes in v2:
time: 186 us
  Pallas kernels  173 us (93%)
  local copies, waits for them, and re-layouts  11.9 us (6%)
    pallas_call x1, Pallas kernels, local_step(): pl.pallas_call(functools.partial(step_kernel, parts), out_shape=outs, in_...  173 us
    unnamed x31, local copies, waits for them, and re-layouts  10.5 us

profile of v2, /device:TPU:0, one launch (start us, length us, event | category | flops | bytes accessed | tf_op | source)
XLA Modules:
  0.0 185.8 jit_solution(9215357176892283732)
XLA Ops:
  0.6 1.4 reshape.31.send_idx
  2.0 173.3 %step.1 = (bf16[2048,256]{1,0:T(8,128)(2,1)}, bf16[2048,256]{1,0:T(8,128)(2,1)}, f32[164,2048]{1,0:T(8,128)}, f32[164,256]{1,0:T(8,128)}, f32[3,256]{1,0:T(4,128...) custom-call(bf16[164,2048]{1,0:T(8,128)(2,1)} %bitcast.7, ...), custom_call_target="tpu_custom_call" | custom-call | tf_op jit(solution)/shard_map/step/pallas_call | solution.py:469
  175.3 0.0 copy-start.2
  175.3 0.0 copy-start.1
  175.3 2.4 %copy.38 = bf16[2048,256]{1,0:T(8,128)(2,1)} copy(bf16[2048,256]{1,0:T(8,128)(2,1)} %get-tuple-element.44) | data formatting | bytes 2097152
  177.8 0.0 copy-done.2
  177.8 1.0 copy.39
  178.7 0.0 copy-done.1
  178.7 0.0 copy-start.6
  178.7 0.0 copy-start.9
  178.7 0.0 copy-start.8
  178.7 0.0 copy-start.3
  178.8 1.1 copy.40
  179.8 0.0 copy-done.6
  179.8 0.0 copy-start.4
  179.8 0.0 copy-start.5
  179.8 0.7 copy.41
  180.5 0.0 copy-done.9
  180.5 0.6 copy.42
  181.1 0.0 copy-done.8
  181.1 0.6 copy.43
  181.7 0.0 copy-done.3
  181.7 0.0 copy-start
  181.7 0.9 copy.44
  182.6 0.0 copy-done.4
  182.6 0.8 copy.45
  183.4 0.0 copy-done.5
  183.4 0.7 copy.46
  184.1 0.0 copy-done
  184.1 0.0 copy-start.7
  184.1 1.1 copy.47
  185.2 0.0 copy-done.7
  185.2 0.6 copy.48
Async XLA Ops:
  175.3 2.4 %copy-start.2 = (bf16[2048,256]{1,0:T(8,128)(2,1)S(1)}, bf16[2048,256]{1,0:T(8,128)(2,1)}, u32[]{:S(2)}) copy-start(bf16[2048,256]{1,0:T(8,128)(2,1)} %get-tuple-element.45) | copy-start | bytes 3145732
  175.3 3.4 %copy-start.1 = (f32[164,2048]{1,0:T(8,128)S(1)}, f32[164,2048]{1,0:T(8,128)}, u32[]{:S(2)}) copy-start(f32[164,2048]{1,0:T(8,128)} %get-tuple-element.24) | copy-start | bytes 4030468
  178.7 1.1 copy-start.6
  178.7 1.8 copy-start.9
  178.7 2.4 %copy-start.8 = (f32[4,256]{1,0:T(4,128)S(1)}, f32[4,256]{1,0:T(4,128)}, u32[]{:S(2)}) copy-start(f32[4,256]{1,0:T(4,128)} %get-tuple-element.49) | copy-start | bytes 12292
  178.7 3.0 %copy-start.3 = (f32[768,256]{1,0:T(8,128)S(1)}, f32[768,256]{1,0:T(8,128)}, u32[]{:S(2)}) copy-start(f32[768,256]{1,0:T(8,128)} %get-tuple-element.50) | copy-start | bytes 2359300
  179.8 2.8 %copy-start.4 = (f32[512,256]{1,0:T(8,128)S(1)}, f32[512,256]{1,0:T(8,128)}, u32[]{:S(2)}) copy-start(f32[512,256]{1,0:T(8,128)} %get-tuple-element.51) | copy-start | bytes 1572868
  179.8 3.5 %copy-start.5 = (f32[256,256]{1,0:T(8,128)S(1)}, f32[256,256]{1,0:T(8,128)}, u32[]{:S(2)}) copy-start(f32[256,256]{1,0:T(8,128)} %get-tuple-element.52) | copy-start | bytes 786436
  181.7 2.4 %copy-start = (f32[6,256,256]{2,1,0:T(8,128)S(1)}, f32[6,256,256]{2,1,0:T(8,128)}, u32[]{:S(2)}) copy-start(f32[6,256,256]{2,1,0:T(8,128)} %get-tuple-element.53) | copy-start | bytes 4718596
  184.1 1.1 copy-start.7

commit v3 on v2

--- a/solution.py
+++ b/solution.py
@@ -12,7 +12,8 @@
 BF = jnp.bfloat16
 F32 = jnp.float32
 MESH = pl.DeviceIdType.MESH
-TILE = 256
+TILE = 1024
+SEND_TILE = 512
 VMEM_LIMIT = 60 * 1024 * 1024
 
 
@@ -59,7 +60,7 @@
         ref[base + j:base + j + 1, :] += d_vec[j]
 
 
-def rows_at(i, size=TILE):
+def rows_at(i, size):
     return pl.ds(pl.multiple_of(i * size, size), size)
 
 
@@ -73,17 +74,18 @@
     return jnp.where(ids == row_idx, 1.0, 0.0).astype(BF)
 
 
-def col_of(idx_ref, i):
+def col_of(row_ref, i, size):
     cols = []
-    for j in range(TILE // 128):
-        row = idx_ref[pl.ds(i * (TILE // 128) + j, 1), :]
+    for j in range(size // 128):
+        row = row_ref[0:1, pl.ds(pl.multiple_of(i * size, size) + j * 128, 128)]
         cols.append(jnp.transpose(jnp.broadcast_to(row, (8, 128)))[:, 0:1])
     return jnp.concatenate(cols, axis=0)
 
 
 def fill_row(idx_ref, row_ref):
+    wide = idx_ref.shape[1]
     for j in range(idx_ref.shape[0]):
-        row_ref[0:1, j * 128:(j + 1) * 128] = idx_ref[j:j + 1, :]
+        row_ref[0:1, j * wide:(j + 1) * wide] = idx_ref[j:j + 1, :]
 
 
 def loop(n, body, events=()):
@@ -177,8 +179,11 @@
     n_feat, n_grid = grid_t.shape
     n_mesh, n_edge, n_slot = mesh_lat.shape[0], edge_lat.shape[0], outgoing.shape[0]
     cap = n_slot // parts
-    per_tile = TILE // cap
+    per_tile = min(SEND_TILE, n_slot) // cap
     n_feat_pad = -(-n_feat // 8) * 8
+    t_send, t_slot = min(SEND_TILE, n_slot), min(SEND_TILE, n_slot)
+    t_grid, t_mesh, t_edge = min(TILE, n_grid), min(TILE, n_mesh), min(TILE, n_edge)
+    n_gt, n_nt, n_et = n_grid // t_grid, n_mesh // t_mesh, n_edge // t_edge
     me = lax.axis_index(AXIS)
     core = lax.rem(me, 2)
     x_at = lax.rem(me // 2, 2)
@@ -213,8 +218,8 @@
     r_wei = r_wmi + 8
     r_vec = r_wei + 8
     refs = (own, out, r_one, r_two, r_three, r_four, red_send, red_recv)
-    bounds = [0, 5 * lat, 9 * lat, 11 * lat, own.shape[0]]
-    red = [Reducer(g, bounds[g], bounds[g + 1] - bounds[g], place, refs) for g in range(4)]
+    bounds = [0, 2 * lat, 5 * lat, 9 * lat, 11 * lat, own.shape[0]]
+    red = [Reducer(g, bounds[g], bounds[g + 1] - bounds[g], place, refs) for g in range(5)]
 
     own[...] = jnp.zeros_like(own)
     fill_row(send_idx, send_row)
@@ -222,10 +227,10 @@
     fill_row(dst_idx, dst_row)
 
     def embed(i):
-        sl = rows_at(i)
+        sl = rows_at(i, t_grid)
         _, emb = mlp_fwd(tn(grid_t[:, sl], w_grid_in[...]), w_two[0], vec[0])
         grid_lat[sl, :] = emb.astype(BF)
-    loop(n_grid // TILE, embed)
+    loop(n_gt, embed)
 
     pl.semaphore_wait(barrier, parts - 1)
 
@@ -255,7 +260,7 @@
             return carry
         lax.fori_loop(1, parts, one, 0)
 
-    slot_tiles = n_slot // TILE
+    slot_tiles = n_slot // t_send
     my_tile = me // per_tile
 
     def turn(i):
@@ -263,8 +268,8 @@
 
     def pick(i):
         tile = turn(i)
-        sl = rows_at(tile)
-        outgoing[sl, :] = nn(hot_cols(col_of(send_idx, tile), n_grid), grid_lat[...]).astype(BF)
+        sl = rows_at(tile, t_send)
+        outgoing[sl, :] = nn(hot_cols(col_of(send_row, tile, t_send), n_grid), grid_lat[...]).astype(BF)
         send_tile(outgoing, incoming, go_send, go_recv, tile)
     loop(slot_tiles, pick)
 
@@ -272,7 +277,7 @@
     loads[1].wait()
 
     def cells(i):
-        sl = rows_at(i)
+        sl = rows_at(i, t_grid)
         here = grid_lat[sl, :]
         saved, upd = mlp_fwd(nn(here, w_grid_up[...]), w_two[5], vec[5])
         grid_out[sl, :] = (here.astype(F32) + upd).astype(BF)
@@ -282,46 +287,51 @@
         own[r_two5:r_two5 + lat, :] += d_two5
         add_vec(own, r_vec + 20, d_vec)
         d_lat[sl, :] = d_top + nt(d_pre, w_grid_up[...])
-    loop(n_grid // TILE, cells)
+    loop(n_gt, cells)
     stores = [pltpu.make_async_copy(a, b, out_sem.at[k]) for k, (a, b) in enumerate([(grid_out, grid_out_h), (mesh_out, mesh_out_h), (d_grid_t, d_grid_t_h)])]
     stores[0].start()
-
-    def nodes_in(i):
-        sl = rows_at(i)
-        _, emb = mlp_fwd(tn(mesh_t[:, sl], w_mesh_in[...]), w_two[1], vec[1])
-        mesh_lat[sl, :] = emb.astype(BF)
-    loop(n_mesh // TILE, nodes_in)
-
-    def edges_in(i):
-        sl = rows_at(i)
-        _, emb = mlp_fwd(tn(edge_t[:, sl], w_edge_in[...]), w_two[2], vec[2])
-        edge_lat[sl, :] = emb.astype(BF)
-        recv_lat[sl, :] = nn(hot_cols(col_of(dst_idx, i), n_mesh), mesh_lat[...]).astype(BF)
-    loop(n_edge // TILE, edges_in)
-
+    red[0].start(0)
     loads[2].wait()
     loads[3].wait()
     loads[4].wait()
+
+    def nodes_in(i):
+        sl = rows_at(i, t_mesh)
+        _, emb = mlp_fwd(tn(mesh_t[:, sl], w_mesh_in[...]), w_two[1], vec[1])
+        here = emb.astype(BF)
+        mesh_lat[sl, :] = here
+        d_mesh_lat[sl, :] = nn(here, w_mesh_up[0:lat, :])
+    loop(n_nt, nodes_in)
+
+    def edges_in(i):
+        sl = rows_at(i, t_edge)
+        _, emb = mlp_fwd(tn(edge_t[:, sl], w_edge_in[...]), w_two[2], vec[2])
+        here = emb.astype(BF)
+        edge_lat[sl, :] = here
+        recv = nn(hot_cols(col_of(dst_row, i, t_edge), n_mesh), mesh_lat[...]).astype(BF)
+        recv_lat[sl, :] = recv
+        act_s[sl, :] = nn(here, w_edge_up[0:lat, :]) + nn(recv, w_edge_up[2 * lat:3 * lat, :])
+    loop(n_et, edges_in)
+
     wait_all(outgoing, incoming, go_send, go_recv)
+    red[0].step(1)()
 
     def edges_fwd(i):
-        sl = rows_at(i)
-        sent = nn(hot_cols(col_of(src_idx, i), n_slot), incoming[...]).astype(BF)
+        sl = rows_at(i, t_edge)
+        sent = nn(hot_cols(col_of(src_row, i, t_edge), n_slot), incoming[...]).astype(BF)
         send_lat[sl, :] = sent
-        here = edge_lat[sl, :]
-        pre = nn(here, w_edge_up[0:lat, :]) + nn(sent, w_edge_up[lat:2 * lat, :]) + nn(recv_lat[sl, :], w_edge_up[2 * lat:3 * lat, :])
-        (act, _, _, normed, inv), upd = mlp_fwd(pre, w_two[3], vec[3])
+        (act, _, _, normed, inv), upd = mlp_fwd(act_s[sl, :] + nn(sent, w_edge_up[lat:2 * lat, :]), w_two[3], vec[3])
         act_s[sl, :] = act
         nrm_s[sl, :] = normed
-        inv_s[sl, :] = jnp.broadcast_to(inv, (TILE, 128))
-        edge_new[sl, :] = (here.astype(F32) + upd).astype(BF)
-    loop(n_edge // TILE, edges_fwd)
+        inv_s[sl, :] = jnp.broadcast_to(inv, (t_edge, 128))
+        edge_new[sl, :] = (edge_lat[sl, :].astype(F32) + upd).astype(BF)
+    loop(n_et, edges_fwd, [(0, red[0].step(2)), (n_et // 2, red[0].step(3)), (n_et - 1, red[0].step(4))])
 
     def nodes(i):
-        sl = rows_at(i)
-        agg = nn(hot_rows(dst_row[...], i * TILE, TILE), edge_new[...]).astype(BF)
+        sl = rows_at(i, t_mesh)
+        agg = nn(hot_rows(dst_row[...], i * t_mesh, t_mesh), edge_new[...]).astype(BF)
         here = mesh_lat[sl, :]
-        saved, upd = mlp_fwd(nn(here, w_mesh_up[0:lat, :]) + nn(agg, w_mesh_up[lat:2 * lat, :]), w_two[4], vec[4])
+        saved, upd = mlp_fwd(d_mesh_lat[sl, :] + nn(agg, w_mesh_up[lat:2 * lat, :]), w_two[4], vec[4])
         mesh_out[sl, :] = (here.astype(F32) + upd).astype(BF)
         d_top = d_mesh[sl, :].astype(F32)
         d_pre, d_two4, d_vec = mlp_bwd(saved, w_two[4], vec[4], d_top)
@@ -331,12 +341,13 @@
         own[r_two4:r_two4 + lat, :] += d_two4
         add_vec(own, r_vec + 16, d_vec)
         d_mesh_lat[sl, :] = d_top + nt(d_pre, w_mesh_up[0:lat, :])
-    loop(n_mesh // TILE, nodes)
+    loop(n_nt, nodes, [(0, red[0].step(5)), (n_nt - 1, red[0].step(6))])
     stores[1].start()
+    red[1].start(0)
 
     def edges_bwd(i):
-        sl = rows_at(i)
-        picked = nn(hot_cols(col_of(dst_idx, i), n_mesh), d_pre4[...]).astype(BF)
+        sl = rows_at(i, t_edge)
+        picked = nn(hot_cols(col_of(dst_row, i, t_edge), n_mesh), d_pre4[...]).astype(BF)
         d_new = nt(picked, w_mesh_up[lat:2 * lat, :])
         act = act_s[sl, :]
         sig = 0.5 * jnp.tanh(0.5 * act) + 0.5
@@ -345,27 +356,30 @@
         d_pre3[sl, :] = d_pre
         own[r_two3:r_two3 + lat, :] += d_two3
         add_vec(own, r_vec + 12, d_vec)
+        d_edge_lat[sl, :] = d_new
+    loop(n_et, edges_bwd, [(0, red[0].step(7)), (0, red[1].step(1)), (n_et // 2, red[0].step(8)), (n_et // 2, red[1].step(2)), (n_et - 1, red[1].step(3))])
+
+    def slots(i):
+        tile = turn(i)
+        sl = rows_at(tile, t_send)
+        d_slot = nn(hot_rows(src_row[...], tile * t_send, t_send), d_pre3[...]).astype(BF)
+        d_incoming[sl, :] = nt(d_slot, w_edge_up[lat:2 * lat, :]).astype(BF)
+        send_tile(d_incoming, d_sent, back_send, back_recv, tile)
+    loop(slot_tiles, slots)
+
+    def edges_grad(i):
+        sl = rows_at(i, t_edge)
+        d_pre = d_pre3[sl, :]
         own[r_weu:r_weu + lat, :] += tn(edge_lat[sl, :], d_pre)
         own[r_weu + lat:r_weu + 2 * lat, :] += tn(send_lat[sl, :], d_pre)
         own[r_weu + 2 * lat:r_weu + 3 * lat, :] += tn(recv_lat[sl, :], d_pre)
-        d_edge_lat[sl, :] = d_new + nt(d_pre, w_edge_up[0:lat, :])
-    n_et, n_nt, n_gt = n_edge // TILE, n_mesh // TILE, n_grid // TILE
-    red[0].start(0)
-    loop(n_et, edges_bwd, [(n_et * 2 // 12, red[0].step(1)), (n_et * 7 // 12, red[0].step(2)), (n_et - 1, red[0].step(3))])
-
-    red[1].start(0)
-
-    def slots(i):
-        tile = turn(i)
-        sl = rows_at(tile)
-        d_slot = nn(hot_rows(src_row[...], tile * TILE, TILE), d_pre3[...]).astype(BF)
-        d_incoming[sl, :] = nt(d_slot, w_edge_up[lat:2 * lat, :]).astype(BF)
-        send_tile(d_incoming, d_sent, back_send, back_recv, tile)
-    loop(slot_tiles, slots, [(slot_tiles - 1, red[1].step(1))])
+        d_edge_lat[sl, :] += nt(d_pre, w_edge_up[0:lat, :])
+    loop(n_et, edges_grad)
+    red[2].start(0)
 
     def nodes_bwd(i):
-        sl = rows_at(i)
-        d_node = nn(hot_rows(dst_row[...], i * TILE, TILE), d_pre3[...]).astype(BF)
+        sl = rows_at(i, t_mesh)
+        d_node = nn(hot_rows(dst_row[...], i * t_mesh, t_mesh), d_pre3[...]).astype(BF)
         d_top = d_mesh_lat[sl, :] + nt(d_node, w_edge_up[2 * lat:3 * lat, :])
         feat = mesh_t[:, sl]
         saved, _ = mlp_fwd(tn(feat, w_mesh_in[...]), w_two[1], vec[1])
@@ -373,25 +387,27 @@
         own[r_two1:r_two1 + lat, :] += d_two1
         own[r_wmi:r_wmi + 3, :] += nn(feat, d_pre)
         add_vec(own, r_vec + 4, d_vec)
-    loop(n_nt, nodes_bwd, [(n_nt * 2 // 8, red[0].step(4)), (n_nt - 1, red[1].step(2))])
+    loop(n_nt, nodes_bwd, [(0, red[2].step(1)), (n_nt - 1, red[2].step(2))])
 
     def edges_in_bwd(i):
-        sl = rows_at(i)
+        sl = rows_at(i, t_edge)
         feat = edge_t[:, sl]
         saved, _ = mlp_fwd(tn(feat, w_edge_in[...]), w_two[2], vec[2])
         d_pre, d_two2, d_vec = mlp_bwd(saved, w_two[2], vec[2], d_edge_lat[sl, :])
         own[r_two2:r_two2 + lat, :] += d_two2
         own[r_wei:r_wei + 4, :] += nn(feat, d_pre)
         add_vec(own, r_vec + 8, d_vec)
-    loop(n_et, edges_in_bwd, [(n_et * 2 // 12, red[0].step(5)), (n_et * 5 // 12, red[1].step(3)), (n_et * 7 // 12, red[0].step(6)), (n_et - 1, red[0].step(7))])
-
-    red[2].start(0)
+    loop(n_et, edges_in_bwd)
+
+    red[3].start(0)
     wait_all(d_incoming, d_sent, back_send, back_recv)
     red[1].step(4)()
+    red[2].step(3)()
+    red[3].step(1)()
 
     def grid_bwd(i):
-        sl = rows_at(i)
-        d_top = d_lat[sl, :] + nn(hot_rows(send_row[...], i * TILE, TILE), d_sent[...])
+        sl = rows_at(i, t_grid)
+        d_top = d_lat[sl, :] + nn(hot_rows(send_row[...], i * t_grid, t_grid), d_sent[...])
         feat = grid_t[:, sl]
         saved, _ = mlp_fwd(tn(feat, w_grid_in[...]), w_two[0], vec[0])
         d_pre, d_two0, d_vec = mlp_bwd(saved, w_two[0], vec[0], d_top)
@@ -399,28 +415,19 @@
         own[r_wgi:r_wgi + n_feat, :] += nn(feat, d_pre)
         add_vec(own, r_vec, d_vec)
         d_grid_t[:, sl] = nt(w_grid_in[...], d_pre)
-    loop(n_gt, grid_bwd, [(0, red[2].step(1)), (n_gt * 2 // 8, red[0].step(8)), (n_gt * 3 // 8, red[1].step(5)), (n_gt * 4 // 8, red[2].step(2)), (n_gt * 5 // 8, red[1].step(6)), (n_gt - 1, red[2].step(3))])
+    loop(n_gt, grid_bwd, [(0, red[1].step(5)), (0, red[2].step(4)), (0, red[3].step(2)), (n_gt - 1, red[1].step(6)), (n_gt - 1, red[2].step(5)), (n_gt - 1, red[3].step(3))])
+
+    red[4].start(0)
     stores[2].start()
-
-    red[3].start(0)
-    red[1].step(7)()
-    red[3].step(1)()
-    red[2].step(4)()
-    red[1].step(8)()
-    red[3].step(2)()
-    red[2].step(5)()
-    red[3].step(3)()
-    red[2].step(6)()
-    red[3].step(4)()
-    red[2].step(7)()
-    red[2].step(8)()
+    for g, k in ((1, 7), (2, 6), (3, 4), (4, 1), (1, 8), (2, 7), (3, 5), (4, 2), (2, 8), (3, 6), (4, 3), (3, 7), (4, 4), (3, 8)):
+        red[g].step(k)()
     puts = [(r_weu, 3 * lat, d_weu), (r_wmu, 2 * lat, d_wmu), (r_wgu, lat, d_wgu), (r_two1, lat, d_two.at[1]),
             (r_two2, lat, d_two.at[2]), (r_two3, lat, d_two.at[3]), (r_two4, lat, d_two.at[4]), (r_two5, lat, d_two.at[5])]
     moves = [pltpu.make_async_copy(out.at[pl.ds(a, n)], ref, out_sem.at[3 + k]) for k, (a, n, ref) in enumerate(puts)]
     for move in moves:
         move.start()
     for k in range(5, 9):
-        red[3].step(k)()
+        red[4].step(k)()
     last = pltpu.make_async_copy(out.at[pl.ds(r_two0, lat)], d_two.at[0], out_sem.at[11])
     last.start()
     d_wgi[...] = out[r_wgi:r_wgi + n_feat, :]
@@ -465,7 +472,7 @@
                    V((n_mesh, lat), BF), V((n_mesh, lat), F32), V((n_edge, lat), F32), V((n_edge, lat), BF), V((n_slot, lat), BF), V((n_slot, lat), BF),
                    V((1, n_slot), jnp.int32), V((1, n_edge), jnp.int32), V((1, n_edge), jnp.int32),
                    V((total, lat), F32), V((total, lat), F32), V((total // 2, lat), F32), V((total // 4, lat), F32), V((total // 8, lat), F32), V((3, total // 32, lat), F32),
-                   D((5,)), D((12,)), D((parts,)), D((parts,)), D((parts,)), D((parts,)), D((4, 12)), D((4, 12))]
+                   D((5,)), D((12,)), D((parts,)), D((parts,)), D((parts,)), D((parts,)), D((5, 12)), D((5, 12))]
         res = pl.pallas_call(
             functools.partial(step_kernel, parts),
             out_shape=outs,
@@ -474,7 +481,7 @@
             scratch_shapes=scratch,
             compiler_params=pltpu.CompilerParams(vmem_limit_bytes=VMEM_LIMIT, collective_id=0, has_side_effects=True),
             name='step',
-        )(grid_in.T, mesh_static.T, edge_static.T, send_rows.reshape(-1, 128), edge_src.reshape(-1, 128), edge_dst.reshape(-1, 128),
+        )(grid_in.T, mesh_static.T, edge_static.T, send_rows, edge_src.reshape(-1, 128), edge_dst.reshape(-1, 128),
           w_grid_in, w_mesh_in, w_edge_in, w_second, vectors, w_edge_up, w_mesh_up, w_grid_up, d_mesh_out, d_grid_out)
         return (res[0], res[1], res[2].T) + tuple(res[3:])
 

time: 186 us -> 154 us (0.83)
  Pallas kernels: 173 us -> 143 us
    pallas_call x1, Pallas kernels: 173 us -> 143 us  [local_step(): pl.pallas_call(functools.partial(step_kernel, parts), out_shape=outs, in_...]
where the time goes in v3:
time: 154 us
  Pallas kernels  143 us (93%)
  local copies, waits for them, and re-layouts  10.5 us (7%)
    pallas_call x1, Pallas kernels, local_step(): pl.pallas_call(functools.partial(step_kernel, parts), out_shape=outs, in_...  143 us
    unnamed x31, local copies, waits for them, and re-layouts  10.5 us

profile of v3, /device:TPU:0, one launch (start us, length us, event | category | flops | bytes accessed | tf_op | source)
XLA Modules:
  0.0 153.9 jit_solution(17767979528209610811)
XLA Ops:
  0.7 142.7 %step.1 = (bf16[2048,256]{1,0:T(8,128)(2,1)}, bf16[2048,256]{1,0:T(8,128)(2,1)}, f32[164,2048]{1,0:T(8,128)}, f32[164,256]{1,0:T(8,128)}, f32[3,256]{1,0:T(4,128...) custom-call(bf16[164,2048]{1,0:T(8,128)(2,1)} %bitcast.7, ...), custom_call_target="tpu_custom_call" | custom-call | tf_op jit(solution)/shard_map/step/pallas_call | solution.py:476
  143.3 0.0 copy-start.2
  143.4 0.0 copy-start.1
  143.4 2.4 %copy.38 = bf16[2048,256]{1,0:T(8,128)(2,1)} copy(bf16[2048,256]{1,0:T(8,128)(2,1)} %get-tuple-element.44) | data formatting | bytes 2097152
  145.8 0.0 copy-done.2
  145.8 1.0 copy.39
  146.8 0.0 copy-done.1
  146.8 0.0 copy-start.6
  146.8 0.0 copy-start.9
  146.8 0.0 copy-start.8
  146.8 0.0 copy-start.3
  146.8 1.1 copy.40
  147.9 0.0 copy-done.6
  147.9 0.0 copy-start.4
  147.9 0.0 copy-start.5
  147.9 0.7 copy.41
  148.5 0.0 copy-done.9
  148.5 0.6 copy.42
  149.1 0.0 copy-done.8
  149.1 0.6 copy.43
  149.7 0.0 copy-done.3
  149.7 0.0 copy-start
  149.7 0.9 copy.44
  150.6 0.0 copy-done.4
  150.6 0.8 copy.45
  151.4 0.0 copy-done.5
  151.4 0.7 copy.46
  152.1 0.0 copy-done
  152.1 0.0 copy-start.7
  152.1 1.1 copy.47
  153.3 0.0 copy-done.7
  153.3 0.6 copy.48
Async XLA Ops:
  143.3 2.4 %copy-start.2 = (bf16[2048,256]{1,0:T(8,128)(2,1)S(1)}, bf16[2048,256]{1,0:T(8,128)(2,1)}, u32[]{:S(2)}) copy-start(bf16[2048,256]{1,0:T(8,128)(2,1)} %get-tuple-element.45) | copy-start | bytes 3145732
  143.4 3.4 %copy-start.1 = (f32[164,2048]{1,0:T(8,128)S(1)}, f32[164,2048]{1,0:T(8,128)}, u32[]{:S(2)}) copy-start(f32[164,2048]{1,0:T(8,128)} %get-tuple-element.24) | copy-start | bytes 4030468
  146.8 1.1 copy-start.6
  146.8 1.8 %copy-start.9 = (f32[3,256]{1,0:T(4,128)S(1)}, f32[3,256]{1,0:T(4,128)}, u32[]{:S(2)}) copy-start(f32[3,256]{1,0:T(4,128)} %get-tuple-element.48) | copy-start | bytes 9220
  146.8 2.4 %copy-start.8 = (f32[4,256]{1,0:T(4,128)S(1)}, f32[4,256]{1,0:T(4,128)}, u32[]{:S(2)}) copy-start(f32[4,256]{1,0:T(4,128)} %get-tuple-element.49) | copy-start | bytes 12292
  146.8 3.0 %copy-start.3 = (f32[768,256]{1,0:T(8,128)S(1)}, f32[768,256]{1,0:T(8,128)}, u32[]{:S(2)}) copy-start(f32[768,256]{1,0:T(8,128)} %get-tuple-element.50) | copy-start | bytes 2359300
  147.9 2.8 %copy-start.4 = (f32[512,256]{1,0:T(8,128)S(1)}, f32[512,256]{1,0:T(8,128)}, u32[]{:S(2)}) copy-start(f32[512,256]{1,0:T(8,128)} %get-tuple-element.51) | copy-start | bytes 1572868
  147.9 3.5 %copy-start.5 = (f32[256,256]{1,0:T(8,128)S(1)}, f32[256,256]{1,0:T(8,128)}, u32[]{:S(2)}) copy-start(f32[256,256]{1,0:T(8,128)} %get-tuple-element.52) | copy-start | bytes 786436
  149.7 2.4 %copy-start = (f32[6,256,256]{2,1,0:T(8,128)S(1)}, f32[6,256,256]{2,1,0:T(8,128)}, u32[]{:S(2)}) copy-start(f32[6,256,256]{2,1,0:T(8,128)} %get-tuple-element.53) | copy-start | bytes 4718596
  152.1 1.1 copy-start.7

commit v4 on v3

--- a/solution.py
+++ b/solution.py
@@ -13,7 +13,6 @@
 F32 = jnp.float32
 MESH = pl.DeviceIdType.MESH
 TILE = 1024
-SEND_TILE = 512
 VMEM_LIMIT = 60 * 1024 * 1024
 
 
@@ -64,22 +63,28 @@
     return pl.ds(pl.multiple_of(i * size, size), size)
 
 
+def one_hot(ids, idx):
+    return jnp.where(ids == idx, 1.0, 0.0).astype(BF)
+
+
 def hot_cols(col_idx, width):
-    ids = lax.broadcasted_iota(jnp.int32, (col_idx.shape[0], width), 1)
-    return jnp.where(ids == col_idx, 1.0, 0.0).astype(BF)
+    return one_hot(lax.broadcasted_iota(jnp.int32, (col_idx.shape[0], width), 1), col_idx)
 
 
 def hot_rows(row_idx, base, height):
-    ids = lax.broadcasted_iota(jnp.int32, (height, row_idx.shape[1]), 0) + base
-    return jnp.where(ids == row_idx, 1.0, 0.0).astype(BF)
-
-
-def col_of(row_ref, i, size):
+    return one_hot(lax.broadcasted_iota(jnp.int32, (height, row_idx.shape[1]), 0) + base, row_idx)
+
+
+def col_of(row_ref, starts):
     cols = []
-    for j in range(size // 128):
-        row = row_ref[0:1, pl.ds(pl.multiple_of(i * size, size) + j * 128, 128)]
+    for start in starts:
+        row = row_ref[0:1, pl.ds(pl.multiple_of(start, 128), 128)]
         cols.append(jnp.transpose(jnp.broadcast_to(row, (8, 128)))[:, 0:1])
     return jnp.concatenate(cols, axis=0)
+
+
+def tile_starts(i, size):
+    return [i * size + j * 128 for j in range(size // 128)]
 
 
 def fill_row(idx_ref, row_ref):
@@ -179,9 +184,8 @@
     n_feat, n_grid = grid_t.shape
     n_mesh, n_edge, n_slot = mesh_lat.shape[0], edge_lat.shape[0], outgoing.shape[0]
     cap = n_slot // parts
-    per_tile = min(SEND_TILE, n_slot) // cap
+    pair = 2 * cap
     n_feat_pad = -(-n_feat // 8) * 8
-    t_send, t_slot = min(SEND_TILE, n_slot), min(SEND_TILE, n_slot)
     t_grid, t_mesh, t_edge = min(TILE, n_grid), min(TILE, n_mesh), min(TILE, n_edge)
     n_gt, n_nt, n_et = n_grid // t_grid, n_mesh // t_mesh, n_edge // t_edge
     me = lax.axis_index(AXIS)
@@ -218,8 +222,8 @@
     r_wei = r_wmi + 8
     r_vec = r_wei + 8
     refs = (own, out, r_one, r_two, r_three, r_four, red_send, red_recv)
-    bounds = [0, 2 * lat, 5 * lat, 9 * lat, 11 * lat, own.shape[0]]
-    red = [Reducer(g, bounds[g], bounds[g + 1] - bounds[g], place, refs) for g in range(5)]
+    bounds = [0, 2 * lat, 5 * lat, 9 * lat, 11 * lat, 12 * lat, own.shape[0]]
+    red = [Reducer(g, bounds[g], bounds[g + 1] - bounds[g], place, refs) for g in range(6)]
 
     own[...] = jnp.zeros_like(own)
     fill_row(send_idx, send_row)
@@ -239,39 +243,60 @@
             src_ref=src.at[pl.ds(pl.multiple_of(to * cap, 8), cap)], dst_ref=dst.at[pl.ds(pl.multiple_of(frm * cap, 8), cap)],
             send_sem=sends.at[to], recv_sem=recvs.at[frm], device_id=(to,), device_id_type=MESH)
 
-    def send_tile(src, dst, sends, recvs, tile):
-        for j in range(per_tile):
-            to = tile * per_tile + j
-
-            @pl.when(to != me)
-            def _():
-                part_copy(src, dst, sends, recvs, to, me).start()
-
-            @pl.when(to == me)
-            def _():
-                own_sl = pl.ds(pl.multiple_of(me * cap, 8), cap)
-                dst[own_sl, :] = src[own_sl, :]
-
-    def wait_all(src, dst, sends, recvs):
-        def one(k, carry):
-            other = lax.rem(me + k, parts)
-            part_copy(src, dst, sends, recvs, other, me).wait_send()
-            part_copy(src, dst, sends, recvs, me, other).wait_recv()
-            return carry
-        lax.fori_loop(1, parts, one, 0)
-
-    slot_tiles = n_slot // t_send
-    my_tile = me // per_tile
-
-    def turn(i):
-        return lax.rem(my_tile + slot_tiles // 2 + i, slot_tiles)
+    z_flip = z_at + 1 - 2 * lax.rem(z_at, 2)
+    z_order = [lax.rem(z_at + 2, 4), z_flip, lax.rem(z_flip + 2, 4), z_at]
+    planes = parts // 8
+
+    def group_of(i):
+        flip_x, flip_y = lax.rem(i + 1, 2), 1 - i // 2
+        return x_at + flip_x * (1 - 2 * x_at) + 2 * (y_at + flip_y * (1 - 2 * y_at))
+
+    def starts_of(group):
+        return [z * 8 * cap + group * pair for z in range(planes)]
+
+    def pair_at(start):
+        return pl.ds(pl.multiple_of(start, 8), pair)
+
+    def send_group(src, dst, sends, recvs, group):
+        for z in z_order:
+            for c in range(2):
+                to = z * 8 + group * 2 + c
+
+                @pl.when(to != me)
+                def _():
+                    part_copy(src, dst, sends, recvs, to, me).start()
+
+                @pl.when(to == me)
+                def _():
+                    own_sl = pl.ds(pl.multiple_of(me * cap, 8), cap)
+                    dst[own_sl, :] = src[own_sl, :]
+
+    def wait_group(src, dst, sends, recvs, group):
+        for z in range(planes):
+            for c in range(2):
+                other = z * 8 + group * 2 + c
+
+                @pl.when(other != me)
+                def _():
+                    part_copy(src, dst, sends, recvs, other, me).wait_send()
+                    part_copy(src, dst, sends, recvs, me, other).wait_recv()
+
+    def put_group(ref, group, rows):
+        for z, start in enumerate(starts_of(group)):
+            ref[pair_at(start), :] = rows[z * pair:(z + 1) * pair]
+
+    def get_group(ref, group):
+        return jnp.concatenate([ref[pair_at(start), :] for start in starts_of(group)], axis=0)
+
+    def spread(ids, group):
+        return ids + (ids // pair) * (8 * cap - pair) + group * pair
 
     def pick(i):
-        tile = turn(i)
-        sl = rows_at(tile, t_send)
-        outgoing[sl, :] = nn(hot_cols(col_of(send_row, tile, t_send), n_grid), grid_lat[...]).astype(BF)
-        send_tile(outgoing, incoming, go_send, go_recv, tile)
-    loop(slot_tiles, pick)
+        group = group_of(i)
+        rows = nn(hot_cols(col_of(send_row, starts_of(group)), n_grid), grid_lat[...]).astype(BF)
+        put_group(outgoing, group, rows)
+        send_group(outgoing, incoming, go_send, go_recv, group)
+    loop(4, pick)
 
     loads[0].wait()
     loads[1].wait()
@@ -308,24 +333,43 @@
         _, emb = mlp_fwd(tn(edge_t[:, sl], w_edge_in[...]), w_two[2], vec[2])
         here = emb.astype(BF)
         edge_lat[sl, :] = here
-        recv = nn(hot_cols(col_of(dst_row, i, t_edge), n_mesh), mesh_lat[...]).astype(BF)
+        recv = nn(hot_cols(col_of(dst_row, tile_starts(i, t_edge)), n_mesh), mesh_lat[...]).astype(BF)
         recv_lat[sl, :] = recv
         act_s[sl, :] = nn(here, w_edge_up[0:lat, :]) + nn(recv, w_edge_up[2 * lat:3 * lat, :])
     loop(n_et, edges_in)
 
-    wait_all(outgoing, incoming, go_send, go_recv)
     red[0].step(1)()
+
+    def gather(i):
+        group = group_of(i // n_et)
+        tile = lax.rem(i, n_et)
+        sl = rows_at(tile, t_edge)
+
+        @pl.when(tile == 0)
+        def _():
+            wait_group(outgoing, incoming, go_send, go_recv, group)
+        ids = spread(lax.broadcasted_iota(jnp.int32, (t_edge, 4 * pair), 1), group)
+        rows = nn(one_hot(ids, col_of(src_row, tile_starts(tile, t_edge))), get_group(incoming, group))
+
+        @pl.when(i < n_et)
+        def _():
+            nrm_s[sl, :] = rows
+
+        @pl.when(i >= n_et)
+        def _():
+            nrm_s[sl, :] += rows
+    loop(4 * n_et, gather, [(n_et - 1, red[0].step(2)), (2 * n_et - 1, red[0].step(3))])
 
     def edges_fwd(i):
         sl = rows_at(i, t_edge)
-        sent = nn(hot_cols(col_of(src_row, i, t_edge), n_slot), incoming[...]).astype(BF)
+        sent = nrm_s[sl, :].astype(BF)
         send_lat[sl, :] = sent
         (act, _, _, normed, inv), upd = mlp_fwd(act_s[sl, :] + nn(sent, w_edge_up[lat:2 * lat, :]), w_two[3], vec[3])
         act_s[sl, :] = act
         nrm_s[sl, :] = normed
         inv_s[sl, :] = jnp.broadcast_to(inv, (t_edge, 128))
         edge_new[sl, :] = (edge_lat[sl, :].astype(F32) + upd).astype(BF)
-    loop(n_et, edges_fwd, [(0, red[0].step(2)), (n_et // 2, red[0].step(3)), (n_et - 1, red[0].step(4))])
+    loop(n_et, edges_fwd, [(0, red[0].step(4)), (n_et - 1, red[0].step(5))])
 
     def nodes(i):
         sl = rows_at(i, t_mesh)
@@ -341,13 +385,13 @@
         own[r_two4:r_two4 + lat, :] += d_two4
         add_vec(own, r_vec + 16, d_vec)
         d_mesh_lat[sl, :] = d_top + nt(d_pre, w_mesh_up[0:lat, :])
-    loop(n_nt, nodes, [(0, red[0].step(5)), (n_nt - 1, red[0].step(6))])
+    loop(n_nt, nodes, [(0, red[0].step(6)), (n_nt - 1, red[0].step(7))])
     stores[1].start()
     red[1].start(0)
 
     def edges_bwd(i):
         sl = rows_at(i, t_edge)
-        picked = nn(hot_cols(col_of(dst_row, i, t_edge), n_mesh), d_pre4[...]).astype(BF)
+        picked = nn(hot_cols(col_of(dst_row, tile_starts(i, t_edge)), n_mesh), d_pre4[...]).astype(BF)
         d_new = nt(picked, w_mesh_up[lat:2 * lat, :])
         act = act_s[sl, :]
         sig = 0.5 * jnp.tanh(0.5 * act) + 0.5
@@ -357,15 +401,15 @@
         own[r_two3:r_two3 + lat, :] += d_two3
         add_vec(own, r_vec + 12, d_vec)
         d_edge_lat[sl, :] = d_new
-    loop(n_et, edges_bwd, [(0, red[0].step(7)), (0, red[1].step(1)), (n_et // 2, red[0].step(8)), (n_et // 2, red[1].step(2)), (n_et - 1, red[1].step(3))])
+    loop(n_et, edges_bwd, [(0, red[0].step(8)), (0, red[1].step(1)), (n_et // 2, red[1].step(2)), (n_et - 1, red[1].step(3))])
 
     def slots(i):
-        tile = turn(i)
-        sl = rows_at(tile, t_send)
-        d_slot = nn(hot_rows(src_row[...], tile * t_send, t_send), d_pre3[...]).astype(BF)
-        d_incoming[sl, :] = nt(d_slot, w_edge_up[lat:2 * lat, :]).astype(BF)
-        send_tile(d_incoming, d_sent, back_send, back_recv, tile)
-    loop(slot_tiles, slots)
+        group = group_of(i)
+        ids = spread(lax.broadcasted_iota(jnp.int32, (4 * pair, n_edge), 0), group)
+        d_slot = nn(one_hot(ids, src_row[...]), d_pre3[...]).astype(BF)
+        put_group(d_incoming, group, nt(d_slot, w_edge_up[lat:2 * lat, :]).astype(BF))
+        send_group(d_incoming, d_sent, back_send, back_recv, group)
+    loop(4, slots)
 
     def edges_grad(i):
         sl = rows_at(i, t_edge)
@@ -387,7 +431,7 @@
         own[r_two1:r_two1 + lat, :] += d_two1
         own[r_wmi:r_wmi + 3, :] += nn(feat, d_pre)
         add_vec(own, r_vec + 4, d_vec)
-    loop(n_nt, nodes_bwd, [(0, red[2].step(1)), (n_nt - 1, red[2].step(2))])
+    loop(n_nt, nodes_bwd, [(0, red[1].step(4)), (0, red[2].step(1)), (n_nt - 1, red[1].step(5)), (n_nt - 1, red[2].step(2))])
 
     def edges_in_bwd(i):
         sl = rows_at(i, t_edge)
@@ -397,17 +441,27 @@
         own[r_two2:r_two2 + lat, :] += d_two2
         own[r_wei:r_wei + 4, :] += nn(feat, d_pre)
         add_vec(own, r_vec + 8, d_vec)
-    loop(n_et, edges_in_bwd)
+    loop(n_et, edges_in_bwd, [(n_et - 1, red[1].step(6))])
 
     red[3].start(0)
-    wait_all(d_incoming, d_sent, back_send, back_recv)
-    red[1].step(4)()
-    red[2].step(3)()
-    red[3].step(1)()
+
+    def scatter(i):
+        group = group_of(i // n_gt)
+        tile = lax.rem(i, n_gt)
+        sl = rows_at(tile, t_grid)
+
+        @pl.when(tile == 0)
+        def _():
+            wait_group(d_incoming, d_sent, back_send, back_recv, group)
+        picks = jnp.concatenate([send_row[0:1, pl.ds(pl.multiple_of(start, 128), pair)] for start in starts_of(group)], axis=1)
+        d_lat[sl, :] += nn(hot_rows(picks, tile * t_grid, t_grid), get_group(d_sent, group))
+    loop(4 * n_gt, scatter, [(n_gt - 1, red[3].step(1)), (2 * n_gt - 1, red[1].step(7)), (3 * n_gt - 1, red[2].step(3))])
+    red[1].step(8)()
+    red[3].step(2)()
 
     def grid_bwd(i):
         sl = rows_at(i, t_grid)
-        d_top = d_lat[sl, :] + nn(hot_rows(send_row[...], i * t_grid, t_grid), d_sent[...])
+        d_top = d_lat[sl, :]
         feat = grid_t[:, sl]
         saved, _ = mlp_fwd(tn(feat, w_grid_in[...]), w_two[0], vec[0])
         d_pre, d_two0, d_vec = mlp_bwd(saved, w_two[0], vec[0], d_top)
@@ -415,11 +469,12 @@
         own[r_wgi:r_wgi + n_feat, :] += nn(feat, d_pre)
         add_vec(own, r_vec, d_vec)
         d_grid_t[:, sl] = nt(w_grid_in[...], d_pre)
-    loop(n_gt, grid_bwd, [(0, red[1].step(5)), (0, red[2].step(4)), (0, red[3].step(2)), (n_gt - 1, red[1].step(6)), (n_gt - 1, red[2].step(5)), (n_gt - 1, red[3].step(3))])
+    loop(n_gt, grid_bwd, [(0, red[2].step(4)), (0, red[3].step(3)), (n_gt - 1, red[2].step(5)), (n_gt - 1, red[3].step(4))])
 
     red[4].start(0)
+    red[5].start(0)
     stores[2].start()
-    for g, k in ((1, 7), (2, 6), (3, 4), (4, 1), (1, 8), (2, 7), (3, 5), (4, 2), (2, 8), (3, 6), (4, 3), (3, 7), (4, 4), (3, 8)):
+    for g, k in ((4, 1), (5, 1), (2, 6), (3, 5), (4, 2), (5, 2), (2, 7), (3, 6), (4, 3), (5, 3), (2, 8), (3, 7), (4, 4), (5, 4), (3, 8)):
         red[g].step(k)()
     puts = [(r_weu, 3 * lat, d_weu), (r_wmu, 2 * lat, d_wmu), (r_wgu, lat, d_wgu), (r_two1, lat, d_two.at[1]),
             (r_two2, lat, d_two.at[2]), (r_two3, lat, d_two.at[3]), (r_two4, lat, d_two.at[4]), (r_two5, lat, d_two.at[5])]
@@ -428,6 +483,7 @@
         move.start()
     for k in range(5, 9):
         red[4].step(k)()
+        red[5].step(k)()
     last = pltpu.make_async_copy(out.at[pl.ds(r_two0, lat)], d_two.at[0], out_sem.at[11])
     last.start()
     d_wgi[...] = out[r_wgi:r_wgi + n_feat, :]
@@ -436,6 +492,20 @@
     for k in range(6):
         d_vec_out[k] = out[r_vec + 4 * k:r_vec + 4 * k + 4, :]
     for copy in stores + moves + [last]:
+        copy.wait()
+
+
+def finish_kernel(*refs):
+    n = (len(refs) - 2) // 3
+    srcs, dsts, held, (in_sem, out_sem) = refs[:n], refs[n:2 * n], refs[2 * n:3 * n], refs[3 * n:]
+    takes = [pltpu.make_async_copy(srcs[k], held[k], in_sem.at[k]) for k in range(n)]
+    gives = [pltpu.make_async_copy(held[k], dsts[k], out_sem.at[k]) for k in range(n)]
+    for copy in takes:
+        copy.start()
+    for take, give in zip(takes, gives):
+        take.wait()
+        give.start()
+    for copy in gives:
         copy.wait()
 
 
@@ -472,7 +542,7 @@
                    V((n_mesh, lat), BF), V((n_mesh, lat), F32), V((n_edge, lat), F32), V((n_edge, lat), BF), V((n_slot, lat), BF), V((n_slot, lat), BF),
                    V((1, n_slot), jnp.int32), V((1, n_edge), jnp.int32), V((1, n_edge), jnp.int32),
                    V((total, lat), F32), V((total, lat), F32), V((total // 2, lat), F32), V((total // 4, lat), F32), V((total // 8, lat), F32), V((3, total // 32, lat), F32),
-                   D((5,)), D((12,)), D((parts,)), D((parts,)), D((parts,)), D((parts,)), D((5, 12)), D((5, 12))]
+                   D((5,)), D((12,)), D((parts,)), D((parts,)), D((parts,)), D((parts,)), D((6, 12)), D((6, 12))]
         res = pl.pallas_call(
             functools.partial(step_kernel, parts),
             out_shape=outs,
@@ -483,6 +553,15 @@
             name='step',
         )(grid_in.T, mesh_static.T, edge_static.T, send_rows, edge_src.reshape(-1, 128), edge_dst.reshape(-1, 128),
           w_grid_in, w_mesh_in, w_edge_in, w_second, vectors, w_edge_up, w_mesh_up, w_grid_up, d_mesh_out, d_grid_out)
+        res = pl.pallas_call(
+            finish_kernel,
+            out_shape=outs,
+            in_specs=[far] * len(outs),
+            out_specs=[far] * len(outs),
+            scratch_shapes=[V(o.shape, o.dtype) for o in outs] + [D((len(outs),)), D((len(outs),))],
+            compiler_params=pltpu.CompilerParams(vmem_limit_bytes=VMEM_LIMIT),
+            name='finish',
+        )(*res)
         return (res[0], res[1], res[2].T) + tuple(res[3:])
 
     return jax.shard_map(local_step, mesh=mesh, in_specs=in_specs, out_specs=out_specs, check_vma=False)

time: 154 us -> 151 us (0.981)
  local copies, waits for them, and re-layouts: 10.5 us -> 0 us
  Pallas kernels: 143 us -> 150 us
    unnamed x31 -> x0, local copies, waits for them, and re-layouts: 10.5 us -> none
    pallas_call x0 -> x1, Pallas kernels: none -> 6.21 us  [local_step(): pl.pallas_call(finish_kernel, out_shape=outs, in_specs=[far] * len(outs),...]
where the time goes in v4:
time: 151 us; the launch traced here: 150 us
  Pallas kernels  150 us (99%)
    pallas_call x1, Pallas kernels, local_step(): pl.pallas_call(functools.partial(step_kernel, parts), out_shape=outs, in_...  143 us
    pallas_call x1, Pallas kernels, local_step(): pl.pallas_call(finish_kernel, out_shape=outs, in_specs=[far] * len(outs),...  6.21 us

profile of v4, /device:TPU:0, one launch (start us, length us, event | category | flops | bytes accessed | tf_op | source)
XLA Modules:
  0.0 150.4 jit_solution(3078166484279606016)
XLA Ops:
  0.7 143.3 %step.1 = (bf16[2048,256]{1,0:T(8,128)(2,1)}, bf16[2048,256]{1,0:T(8,128)(2,1)}, f32[164,2048]{1,0:T(8,128)}, f32[164,256]{1,0:T(8,128)}, f32[3,256]{1,0:T(4,128...) custom-call(bf16[164,2048]{1,0:T(8,128)(2,1)} %bitcast.6, ...), custom_call_target="tpu_custom_call" | custom-call | tf_op jit(solution)/shard_map/step/pallas_call | solution.py:546
  144.0 6.2 %finish.1 = (bf16[2048,256]{1,0:T(8,128)(2,1)}, bf16[2048,256]{1,0:T(8,128)(2,1)}, f32[164,2048]{1,0:T(8,128)}, f32[164,256]{1,0:T(8,128)}, f32[3,256]{1,0:T(4,1...) custom-call(bf16[2048,256]{1,0:T(8,128)(2,1)} %get-tuple-element.33., ...), custom_call_target="tpu_custom_call" | custom-call | tf_op jit(solution)/shard_map/finish/pallas_call | solution.py:556

commit v5 on v4

--- a/solution.py
+++ b/solution.py
@@ -179,12 +179,13 @@
                 grid_lat, outgoing, incoming, d_lat, mesh_lat, edge_lat, recv_lat, send_lat, edge_new, act_s, nrm_s, inv_s,
                 d_pre4, d_mesh_lat, d_edge_lat, d_pre3, d_incoming, d_sent, send_row, src_row, dst_row,
                 own, out, r_one, r_two, r_three, r_four,
-                in_sem, out_sem, go_send, go_recv, back_send, back_recv, red_send, red_recv):
+                in_sem, out_sem, go_send, go_recv, back_send, back_recv, red_send, red_recv,
+                held_go, held_back, zg_send, zg_recv, zb_send, zb_recv):
     lat = w_two.shape[1]
     n_feat, n_grid = grid_t.shape
     n_mesh, n_edge, n_slot = mesh_lat.shape[0], edge_lat.shape[0], outgoing.shape[0]
     cap = n_slot // parts
-    pair = 2 * cap
+    block = n_slot // 4
     n_feat_pad = -(-n_feat // 8) * 8
     t_grid, t_mesh, t_edge = min(TILE, n_grid), min(TILE, n_mesh), min(TILE, n_edge)
     n_gt, n_nt, n_et = n_grid // t_grid, n_mesh // t_mesh, n_edge // t_edge
@@ -238,64 +239,71 @@
 
     pl.semaphore_wait(barrier, parts - 1)
 
-    def part_copy(src, dst, sends, recvs, to, frm):
-        return pltpu.make_async_remote_copy(
-            src_ref=src.at[pl.ds(pl.multiple_of(to * cap, 8), cap)], dst_ref=dst.at[pl.ds(pl.multiple_of(frm * cap, 8), cap)],
-            send_sem=sends.at[to], recv_sem=recvs.at[frm], device_id=(to,), device_id_type=MESH)
-
-    z_flip = z_at + 1 - 2 * lax.rem(z_at, 2)
-    z_order = [lax.rem(z_at + 2, 4), z_flip, lax.rem(z_flip + 2, 4), z_at]
-    planes = parts // 8
-
-    def group_of(i):
-        flip_x, flip_y = lax.rem(i + 1, 2), 1 - i // 2
-        return x_at + flip_x * (1 - 2 * x_at) + 2 * (y_at + flip_y * (1 - 2 * y_at))
-
-    def starts_of(group):
-        return [z * 8 * cap + group * pair for z in range(planes)]
-
-    def pair_at(start):
-        return pl.ds(pl.multiple_of(start, 8), pair)
-
-    def send_group(src, dst, sends, recvs, group):
-        for z in z_order:
-            for c in range(2):
-                to = z * 8 + group * 2 + c
-
-                @pl.when(to != me)
-                def _():
-                    part_copy(src, dst, sends, recvs, to, me).start()
-
-                @pl.when(to == me)
-                def _():
-                    own_sl = pl.ds(pl.multiple_of(me * cap, 8), cap)
-                    dst[own_sl, :] = src[own_sl, :]
-
-    def wait_group(src, dst, sends, recvs, group):
-        for z in range(planes):
-            for c in range(2):
-                other = z * 8 + group * 2 + c
-
-                @pl.when(other != me)
-                def _():
-                    part_copy(src, dst, sends, recvs, other, me).wait_send()
-                    part_copy(src, dst, sends, recvs, me, other).wait_recv()
-
-    def put_group(ref, group, rows):
-        for z, start in enumerate(starts_of(group)):
-            ref[pair_at(start), :] = rows[z * pair:(z + 1) * pair]
-
-    def get_group(ref, group):
-        return jnp.concatenate([ref[pair_at(start), :] for start in starts_of(group)], axis=0)
-
-    def spread(ids, group):
-        return ids + (ids // pair) * (8 * cap - pair) + group * pair
+    spot = me - 8 * z_at
+    near = z_at + 1 - 2 * lax.rem(z_at, 2)
+    inner = lax.rem(lax.rem(z_at, 2) + z_at // 2, 2)
+    mid = inner * (3 - z_at) + (1 - inner) * lax.rem(z_at + 2, 4)
+    far = 6 - z_at - near - mid
+
+    def plane_turn(k):
+        return lax.rem(z_at + 4 + (1 - 2 * (z_at // 2)) * (1 + k), 4)
+
+    def block_at(z):
+        return pl.ds(pl.multiple_of(z * block, block), block)
+
+    def cap_at(k):
+        return pl.ds(pl.multiple_of(k * cap, cap), cap)
+
+    class Exchange:
+        def __init__(self, src, held, dst, sems):
+            self.src, self.held, self.dst = src, held, dst
+            self.z_send, self.z_recv, self.p_send, self.p_recv = sems
+
+        def plane_copy(self, to, frm):
+            return pltpu.make_async_remote_copy(src_ref=self.src.at[block_at(to)], dst_ref=self.held.at[block_at(frm)],
+                                                send_sem=self.z_send.at[to], recv_sem=self.z_recv.at[frm], device_id=(spot + 8 * to,), device_id_type=MESH)
+
+        def list_copy(self, src, z, j_to, j_from):
+            return pltpu.make_async_remote_copy(src_ref=src.at[cap_at(z * 8 + j_to)], dst_ref=self.dst.at[cap_at(z * 8 + j_from)],
+                                                send_sem=self.p_send.at[z * 8 + j_to], recv_sem=self.p_recv.at[z * 8 + j_from], device_id=(z_at * 8 + j_to,), device_id_type=MESH)
+
+        def send_lists(self, src, z):
+            for k in range(1, 8):
+                self.list_copy(src, z, lax.rem(spot + k, 8), spot).start()
+            self.dst[cap_at(z * 8 + spot), :] = src[cap_at(z * 8 + spot), :]
+
+        def send_plane(self, z):
+            @pl.when(z != z_at)
+            def _():
+                self.plane_copy(z, z_at).start()
+
+            @pl.when(z == z_at)
+            def _():
+                self.send_lists(self.src, z_at)
+
+        def relay(self, z):
+            def fn():
+                self.plane_copy(z_at, z).wait_recv()
+                self.send_lists(self.held, z)
+            return fn
+
+        def wait_lists(self, z):
+            for k in range(1, 8):
+                j = lax.rem(spot + k, 8)
+                self.list_copy(self.held, z, j, spot).wait_send()
+                self.list_copy(self.held, z, spot, j).wait_recv()
+
+        def wait_planes(self):
+            for z in (near, mid, far):
+                self.plane_copy(z, z_at).wait_send()
+
+    go = Exchange(outgoing, held_go, incoming, (zg_send, zg_recv, go_send, go_recv))
+    back = Exchange(d_incoming, held_back, d_sent, (zb_send, zb_recv, back_send, back_recv))
 
     def pick(i):
-        group = group_of(i)
-        rows = nn(hot_cols(col_of(send_row, starts_of(group)), n_grid), grid_lat[...]).astype(BF)
-        put_group(outgoing, group, rows)
-        send_group(outgoing, incoming, go_send, go_recv, group)
+        z = plane_turn(i)
+        outgoing[block_at(z), :] = nn(hot_cols(col_of(send_row, tile_starts(z, block)), n_grid), grid_lat[...]).astype(BF)
+        go.send_plane(z)
     loop(4, pick)
 
     loads[0].wait()
@@ -312,10 +320,9 @@
         own[r_two5:r_two5 + lat, :] += d_two5
         add_vec(own, r_vec + 20, d_vec)
         d_lat[sl, :] = d_top + nt(d_pre, w_grid_up[...])
-    loop(n_gt, cells)
+    loop(n_gt, cells, [(n_gt - 1, go.relay(near))])
     stores = [pltpu.make_async_copy(a, b, out_sem.at[k]) for k, (a, b) in enumerate([(grid_out, grid_out_h), (mesh_out, mesh_out_h), (d_grid_t, d_grid_t_h)])]
     stores[0].start()
-    red[0].start(0)
     loads[2].wait()
     loads[3].wait()
     loads[4].wait()
@@ -336,29 +343,25 @@
         recv = nn(hot_cols(col_of(dst_row, tile_starts(i, t_edge)), n_mesh), mesh_lat[...]).astype(BF)
         recv_lat[sl, :] = recv
         act_s[sl, :] = nn(here, w_edge_up[0:lat, :]) + nn(recv, w_edge_up[2 * lat:3 * lat, :])
-    loop(n_et, edges_in)
-
-    red[0].step(1)()
-
-    def gather(i):
-        group = group_of(i // n_et)
-        tile = lax.rem(i, n_et)
-        sl = rows_at(tile, t_edge)
-
-        @pl.when(tile == 0)
-        def _():
-            wait_group(outgoing, incoming, go_send, go_recv, group)
-        ids = spread(lax.broadcasted_iota(jnp.int32, (t_edge, 4 * pair), 1), group)
-        rows = nn(one_hot(ids, col_of(src_row, tile_starts(tile, t_edge))), get_group(incoming, group))
-
-        @pl.when(i < n_et)
-        def _():
-            nrm_s[sl, :] = rows
-
-        @pl.when(i >= n_et)
-        def _():
-            nrm_s[sl, :] += rows
-    loop(4 * n_et, gather, [(n_et - 1, red[0].step(2)), (2 * n_et - 1, red[0].step(3))])
+    loop(n_et, edges_in, [(n_et - 1, go.relay(mid))])
+
+
+    def gather(z, first):
+        go.wait_lists(z)
+
+        def fn(i):
+            sl = rows_at(i, t_edge)
+            ids = lax.broadcasted_iota(jnp.int32, (t_edge, block), 1) + z * block
+            rows = nn(one_hot(ids, col_of(src_row, tile_starts(i, t_edge))), incoming[block_at(z), :])
+            nrm_s[sl, :] = rows if first else nrm_s[sl, :] + rows
+        loop(n_et, fn)
+    gather(z_at, True)
+    gather(near, False)
+    go.relay(far)()
+    gather(mid, False)
+    gather(far, False)
+    go.wait_planes()
+    red[0].start(0)
 
     def edges_fwd(i):
         sl = rows_at(i, t_edge)
@@ -369,7 +372,7 @@
         nrm_s[sl, :] = normed
         inv_s[sl, :] = jnp.broadcast_to(inv, (t_edge, 128))
         edge_new[sl, :] = (edge_lat[sl, :].astype(F32) + upd).astype(BF)
-    loop(n_et, edges_fwd, [(0, red[0].step(4)), (n_et - 1, red[0].step(5))])
+    loop(n_et, edges_fwd, [(n_et // 2, red[0].step(1))])
 
     def nodes(i):
         sl = rows_at(i, t_mesh)
@@ -385,7 +388,7 @@
         own[r_two4:r_two4 + lat, :] += d_two4
         add_vec(own, r_vec + 16, d_vec)
         d_mesh_lat[sl, :] = d_top + nt(d_pre, w_mesh_up[0:lat, :])
-    loop(n_nt, nodes, [(0, red[0].step(6)), (n_nt - 1, red[0].step(7))])
+    loop(n_nt, nodes, [(0, red[0].step(2)), (n_nt - 1, red[0].step(3))])
     stores[1].start()
     red[1].start(0)
 
@@ -401,15 +404,15 @@
         own[r_two3:r_two3 + lat, :] += d_two3
         add_vec(own, r_vec + 12, d_vec)
         d_edge_lat[sl, :] = d_new
-    loop(n_et, edges_bwd, [(0, red[0].step(8)), (0, red[1].step(1)), (n_et // 2, red[1].step(2)), (n_et - 1, red[1].step(3))])
+    loop(n_et, edges_bwd, [(0, red[1].step(1)), (0, red[0].step(4)), (n_et // 2, red[1].step(2)), (n_et // 2, red[0].step(5)), (n_et - 1, red[1].step(3)), (n_et - 1, red[0].step(6))])
 
     def slots(i):
-        group = group_of(i)
-        ids = spread(lax.broadcasted_iota(jnp.int32, (4 * pair, n_edge), 0), group)
-        d_slot = nn(one_hot(ids, src_row[...]), d_pre3[...]).astype(BF)
-        put_group(d_incoming, group, nt(d_slot, w_edge_up[lat:2 * lat, :]).astype(BF))
-        send_group(d_incoming, d_sent, back_send, back_recv, group)
+        z = plane_turn(i)
+        d_slot = nn(hot_rows(src_row[...], z * block, block), d_pre3[...]).astype(BF)
+        d_incoming[block_at(z), :] = nt(d_slot, w_edge_up[lat:2 * lat, :]).astype(BF)
+        back.send_plane(z)
     loop(4, slots)
+    red[0].step(7)()
 
     def edges_grad(i):
         sl = rows_at(i, t_edge)
@@ -419,6 +422,7 @@
         own[r_weu + 2 * lat:r_weu + 3 * lat, :] += tn(recv_lat[sl, :], d_pre)
         d_edge_lat[sl, :] += nt(d_pre, w_edge_up[0:lat, :])
     loop(n_et, edges_grad)
+    red[0].step(8)()
     red[2].start(0)
 
     def nodes_bwd(i):
@@ -431,7 +435,7 @@
         own[r_two1:r_two1 + lat, :] += d_two1
         own[r_wmi:r_wmi + 3, :] += nn(feat, d_pre)
         add_vec(own, r_vec + 4, d_vec)
-    loop(n_nt, nodes_bwd, [(0, red[1].step(4)), (0, red[2].step(1)), (n_nt - 1, red[1].step(5)), (n_nt - 1, red[2].step(2))])
+    loop(n_nt, nodes_bwd, [(0, back.relay(near)), (0, red[2].step(1)), (n_nt - 1, red[2].step(2))])
 
     def edges_in_bwd(i):
         sl = rows_at(i, t_edge)
@@ -441,23 +445,27 @@
         own[r_two2:r_two2 + lat, :] += d_two2
         own[r_wei:r_wei + 4, :] += nn(feat, d_pre)
         add_vec(own, r_vec + 8, d_vec)
-    loop(n_et, edges_in_bwd, [(n_et - 1, red[1].step(6))])
-
+    loop(n_et, edges_in_bwd, [(n_et // 2, back.relay(mid))])
     red[3].start(0)
 
-    def scatter(i):
-        group = group_of(i // n_gt)
-        tile = lax.rem(i, n_gt)
-        sl = rows_at(tile, t_grid)
-
-        @pl.when(tile == 0)
-        def _():
-            wait_group(d_incoming, d_sent, back_send, back_recv, group)
-        picks = jnp.concatenate([send_row[0:1, pl.ds(pl.multiple_of(start, 128), pair)] for start in starts_of(group)], axis=1)
-        d_lat[sl, :] += nn(hot_rows(picks, tile * t_grid, t_grid), get_group(d_sent, group))
-    loop(4 * n_gt, scatter, [(n_gt - 1, red[3].step(1)), (2 * n_gt - 1, red[1].step(7)), (3 * n_gt - 1, red[2].step(3))])
-    red[1].step(8)()
-    red[3].step(2)()
+
+    def scatter(z):
+        back.wait_lists(z)
+
+        def fn(i):
+            sl = rows_at(i, t_grid)
+            picks = send_row[0:1, block_at(z)]
+            d_lat[sl, :] += nn(hot_rows(picks, i * t_grid, t_grid), d_sent[block_at(z), :])
+        loop(n_gt, fn)
+    scatter(z_at)
+    scatter(near)
+    red[3].step(1)()
+    back.relay(far)()
+    red[1].step(4)()
+    red[2].step(3)()
+    scatter(mid)
+    scatter(far)
+    back.wait_planes()
 
     def grid_bwd(i):
         sl = rows_at(i, t_grid)
@@ -469,19 +477,20 @@
         own[r_wgi:r_wgi + n_feat, :] += nn(feat, d_pre)
         add_vec(own, r_vec, d_vec)
         d_grid_t[:, sl] = nt(w_grid_in[...], d_pre)
-    loop(n_gt, grid_bwd, [(0, red[2].step(4)), (0, red[3].step(3)), (n_gt - 1, red[2].step(5)), (n_gt - 1, red[3].step(4))])
-
+    loop(n_gt, grid_bwd, [(0, red[1].step(5)), (0, red[2].step(4)), (0, red[3].step(2)), (n_gt - 1, red[1].step(6)), (n_gt - 1, red[3].step(3))])
     red[4].start(0)
     red[5].start(0)
+
     stores[2].start()
-    for g, k in ((4, 1), (5, 1), (2, 6), (3, 5), (4, 2), (5, 2), (2, 7), (3, 6), (4, 3), (5, 3), (2, 8), (3, 7), (4, 4), (5, 4), (3, 8)):
+    for g, k in ((4, 1), (5, 1), (1, 7), (2, 5), (4, 2), (5, 2), (3, 4), (1, 8), (2, 6), (4, 3), (5, 3), (3, 5), (2, 7), (4, 4), (5, 4), (3, 6), (2, 8), (3, 7),
+                 (4, 5), (5, 5), (3, 8)):
         red[g].step(k)()
     puts = [(r_weu, 3 * lat, d_weu), (r_wmu, 2 * lat, d_wmu), (r_wgu, lat, d_wgu), (r_two1, lat, d_two.at[1]),
             (r_two2, lat, d_two.at[2]), (r_two3, lat, d_two.at[3]), (r_two4, lat, d_two.at[4]), (r_two5, lat, d_two.at[5])]
     moves = [pltpu.make_async_copy(out.at[pl.ds(a, n)], ref, out_sem.at[3 + k]) for k, (a, n, ref) in enumerate(puts)]
     for move in moves:
         move.start()
-    for k in range(5, 9):
+    for k in range(6, 9):
         red[4].step(k)()
         red[5].step(k)()
     last = pltpu.make_async_copy(out.at[pl.ds(r_two0, lat)], d_two.at[0], out_sem.at[11])
@@ -542,7 +551,8 @@
                    V((n_mesh, lat), BF), V((n_mesh, lat), F32), V((n_edge, lat), F32), V((n_edge, lat), BF), V((n_slot, lat), BF), V((n_slot, lat), BF),
                    V((1, n_slot), jnp.int32), V((1, n_edge), jnp.int32), V((1, n_edge), jnp.int32),
                    V((total, lat), F32), V((total, lat), F32), V((total // 2, lat), F32), V((total // 4, lat), F32), V((total // 8, lat), F32), V((3, total // 32, lat), F32),
-                   D((5,)), D((12,)), D((parts,)), D((parts,)), D((parts,)), D((parts,)), D((6, 12)), D((6, 12))]
+                   D((5,)), D((12,)), D((parts,)), D((parts,)), D((parts,)), D((parts,)), D((6, 12)), D((6, 12)),
+                   V((n_slot, lat), BF), V((n_slot, lat), BF), D((4,)), D((4,)), D((4,)), D((4,))]
         res = pl.pallas_call(
             functools.partial(step_kernel, parts),
             out_shape=outs,

time: 151 us -> 149 us (0.987)
  Pallas kernels: 150 us -> 148 us
where the time goes in v5:
time: 149 us
  Pallas kernels  148 us (99%)
    pallas_call x1, Pallas kernels, local_step(): pl.pallas_call(functools.partial(step_kernel, parts), out_shape=outs, in_...  142 us
    pallas_call x1, Pallas kernels, local_step(): pl.pallas_call(finish_kernel, out_shape=outs, in_specs=[far] * len(outs),...  6.21 us

profile of v5, /device:TPU:0, one launch (start us, length us, event | category | flops | bytes accessed | tf_op | source)
XLA Modules:
  0.0 149.1 jit_solution(9255716955907963555)
XLA Ops:
  0.7 142.1 %step.1 = (bf16[2048,256]{1,0:T(8,128)(2,1)}, bf16[2048,256]{1,0:T(8,128)(2,1)}, f32[164,2048]{1,0:T(8,128)}, f32[164,256]{1,0:T(8,128)}, f32[3,256]{1,0:T(4,128...) custom-call(bf16[164,2048]{1,0:T(8,128)(2,1)} %bitcast.6, ...), custom_call_target="tpu_custom_call" | custom-call | tf_op jit(solution)/shard_map/step/pallas_call | solution.py:556
  142.7 6.2 %finish.1 = (bf16[2048,256]{1,0:T(8,128)(2,1)}, bf16[2048,256]{1,0:T(8,128)(2,1)}, f32[164,2048]{1,0:T(8,128)}, f32[164,256]{1,0:T(8,128)}, f32[3,256]{1,0:T(4,1...) custom-call(bf16[2048,256]{1,0:T(8,128)(2,1)} %get-tuple-element.33., ...), custom_call_target="tpu_custom_call" | custom-call | tf_op jit(solution)/shard_map/finish/pallas_call | solution.py:566

commit v6 on v4

--- a/solution.py
+++ b/solution.py
@@ -315,7 +315,6 @@
     loop(n_gt, cells)
     stores = [pltpu.make_async_copy(a, b, out_sem.at[k]) for k, (a, b) in enumerate([(grid_out, grid_out_h), (mesh_out, mesh_out_h), (d_grid_t, d_grid_t_h)])]
     stores[0].start()
-    red[0].start(0)
     loads[2].wait()
     loads[3].wait()
     loads[4].wait()
@@ -338,7 +337,6 @@
         act_s[sl, :] = nn(here, w_edge_up[0:lat, :]) + nn(recv, w_edge_up[2 * lat:3 * lat, :])
     loop(n_et, edges_in)
 
-    red[0].step(1)()
 
     def gather(i):
         group = group_of(i // n_et)
@@ -358,7 +356,8 @@
         @pl.when(i >= n_et)
         def _():
             nrm_s[sl, :] += rows
-    loop(4 * n_et, gather, [(n_et - 1, red[0].step(2)), (2 * n_et - 1, red[0].step(3))])
+    loop(4 * n_et, gather)
+    red[0].start(0)
 
     def edges_fwd(i):
         sl = rows_at(i, t_edge)
@@ -369,7 +368,7 @@
         nrm_s[sl, :] = normed
         inv_s[sl, :] = jnp.broadcast_to(inv, (t_edge, 128))
         edge_new[sl, :] = (edge_lat[sl, :].astype(F32) + upd).astype(BF)
-    loop(n_et, edges_fwd, [(0, red[0].step(4)), (n_et - 1, red[0].step(5))])
+    loop(n_et, edges_fwd, [(n_et // 2, red[0].step(1))])
 
     def nodes(i):
         sl = rows_at(i, t_mesh)
@@ -385,7 +384,7 @@
         own[r_two4:r_two4 + lat, :] += d_two4
         add_vec(own, r_vec + 16, d_vec)
         d_mesh_lat[sl, :] = d_top + nt(d_pre, w_mesh_up[0:lat, :])
-    loop(n_nt, nodes, [(0, red[0].step(6)), (n_nt - 1, red[0].step(7))])
+    loop(n_nt, nodes, [(0, red[0].step(2)), (n_nt - 1, red[0].step(3))])
     stores[1].start()
     red[1].start(0)
 
@@ -401,7 +400,7 @@
         own[r_two3:r_two3 + lat, :] += d_two3
         add_vec(own, r_vec + 12, d_vec)
         d_edge_lat[sl, :] = d_new
-    loop(n_et, edges_bwd, [(0, red[0].step(8)), (0, red[1].step(1)), (n_et // 2, red[1].step(2)), (n_et - 1, red[1].step(3))])
+    loop(n_et, edges_bwd, [(0, red[1].step(1)), (0, red[0].step(4)), (n_et // 2, red[1].step(2)), (n_et // 2, red[0].step(5)), (n_et - 1, red[1].step(3)), (n_et - 1, red[0].step(6))])
 
     def slots(i):
         group = group_of(i)
@@ -410,6 +409,7 @@
         put_group(d_incoming, group, nt(d_slot, w_edge_up[lat:2 * lat, :]).astype(BF))
         send_group(d_incoming, d_sent, back_send, back_recv, group)
     loop(4, slots)
+    red[0].step(7)()
 
     def edges_grad(i):
         sl = rows_at(i, t_edge)
@@ -419,6 +419,7 @@
         own[r_weu + 2 * lat:r_weu + 3 * lat, :] += tn(recv_lat[sl, :], d_pre)
         d_edge_lat[sl, :] += nt(d_pre, w_edge_up[0:lat, :])
     loop(n_et, edges_grad)
+    red[0].step(8)()
     red[2].start(0)
 
     def nodes_bwd(i):
@@ -431,7 +432,7 @@
         own[r_two1:r_two1 + lat, :] += d_two1
         own[r_wmi:r_wmi + 3, :] += nn(feat, d_pre)
         add_vec(own, r_vec + 4, d_vec)
-    loop(n_nt, nodes_bwd, [(0, red[1].step(4)), (0, red[2].step(1)), (n_nt - 1, red[1].step(5)), (n_nt - 1, red[2].step(2))])
+    loop(n_nt, nodes_bwd)
 
     def edges_in_bwd(i):
         sl = rows_at(i, t_edge)
@@ -441,9 +442,9 @@
         own[r_two2:r_two2 + lat, :] += d_two2
         own[r_wei:r_wei + 4, :] += nn(feat, d_pre)
         add_vec(own, r_vec + 8, d_vec)
-    loop(n_et, edges_in_bwd, [(n_et - 1, red[1].step(6))])
-
+    loop(n_et, edges_in_bwd)
     red[3].start(0)
+
 
     def scatter(i):
         group = group_of(i // n_gt)
@@ -455,9 +456,7 @@
             wait_group(d_incoming, d_sent, back_send, back_recv, group)
         picks = jnp.concatenate([send_row[0:1, pl.ds(pl.multiple_of(start, 128), pair)] for start in starts_of(group)], axis=1)
         d_lat[sl, :] += nn(hot_rows(picks, tile * t_grid, t_grid), get_group(d_sent, group))
-    loop(4 * n_gt, scatter, [(n_gt - 1, red[3].step(1)), (2 * n_gt - 1, red[1].step(7)), (3 * n_gt - 1, red[2].step(3))])
-    red[1].step(8)()
-    red[3].step(2)()
+    loop(4 * n_gt, scatter, [(3 * n_gt - 1, red[1].step(4)), (3 * n_gt - 1, red[2].step(1)), (3 * n_gt - 1, red[3].step(1))])
 
     def grid_bwd(i):
         sl = rows_at(i, t_grid)
@@ -469,19 +468,20 @@
         own[r_wgi:r_wgi + n_feat, :] += nn(feat, d_pre)
         add_vec(own, r_vec, d_vec)
         d_grid_t[:, sl] = nt(w_grid_in[...], d_pre)
-    loop(n_gt, grid_bwd, [(0, red[2].step(4)), (0, red[3].step(3)), (n_gt - 1, red[2].step(5)), (n_gt - 1, red[3].step(4))])
-
+    loop(n_gt, grid_bwd, [(0, red[2].step(2)), (0, red[3].step(2)), (0, red[1].step(5)), (n_gt - 1, red[2].step(3)), (n_gt - 1, red[3].step(3)), (n_gt - 1, red[1].step(6))])
     red[4].start(0)
     red[5].start(0)
+
     stores[2].start()
-    for g, k in ((4, 1), (5, 1), (2, 6), (3, 5), (4, 2), (5, 2), (2, 7), (3, 6), (4, 3), (5, 3), (2, 8), (3, 7), (4, 4), (5, 4), (3, 8)):
+    for g, k in ((4, 1), (5, 1), (1, 7), (4, 2), (5, 2), (2, 4), (3, 4), (1, 8), (4, 3), (5, 3), (2, 5), (3, 5), (4, 4), (5, 4), (2, 6), (3, 6),
+                 (4, 5), (5, 5), (2, 7), (3, 7), (4, 6), (5, 6), (2, 8), (3, 8)):
         red[g].step(k)()
     puts = [(r_weu, 3 * lat, d_weu), (r_wmu, 2 * lat, d_wmu), (r_wgu, lat, d_wgu), (r_two1, lat, d_two.at[1]),
             (r_two2, lat, d_two.at[2]), (r_two3, lat, d_two.at[3]), (r_two4, lat, d_two.at[4]), (r_two5, lat, d_two.at[5])]
     moves = [pltpu.make_async_copy(out.at[pl.ds(a, n)], ref, out_sem.at[3 + k]) for k, (a, n, ref) in enumerate(puts)]
     for move in moves:
         move.start()
-    for k in range(5, 9):
+    for k in range(7, 9):
         red[4].step(k)()
         red[5].step(k)()
     last = pltpu.make_async_copy(out.at[pl.ds(r_two0, lat)], d_two.at[0], out_sem.at[11])

time: 151 us -> 144 us (0.954)
  Pallas kernels: 150 us -> 143 us
    pallas_call x1, Pallas kernels: 143 us -> 137 us  [local_step(): pl.pallas_call(functools.partial(step_kernel, parts), out_shape=outs, in_...]
where the time goes in v6:
time: 144 us
  Pallas kernels  143 us (99%)
    pallas_call x1, Pallas kernels, local_step(): pl.pallas_call(functools.partial(step_kernel, parts), out_shape=outs, in_...  137 us
    pallas_call x1, Pallas kernels, local_step(): pl.pallas_call(finish_kernel, out_shape=outs, in_specs=[far] * len(outs),...  6.21 us

profile of v6, /device:TPU:0, one launch (start us, length us, event | category | flops | bytes accessed | tf_op | source)
XLA Modules:
  0.0 143.8 jit_solution(11736329927700627991)
XLA Ops:
  0.7 136.7 %step.1 = (bf16[2048,256]{1,0:T(8,128)(2,1)}, bf16[2048,256]{1,0:T(8,128)(2,1)}, f32[164,2048]{1,0:T(8,128)}, f32[164,256]{1,0:T(8,128)}, f32[3,256]{1,0:T(4,128...) custom-call(bf16[164,2048]{1,0:T(8,128)(2,1)} %bitcast.6, ...), custom_call_target="tpu_custom_call" | custom-call | tf_op jit(solution)/shard_map/step/pallas_call | solution.py:546
  137.4 6.2 %finish.1 = (bf16[2048,256]{1,0:T(8,128)(2,1)}, bf16[2048,256]{1,0:T(8,128)(2,1)}, f32[164,2048]{1,0:T(8,128)}, f32[164,256]{1,0:T(8,128)}, f32[3,256]{1,0:T(4,1...) custom-call(bf16[2048,256]{1,0:T(8,128)(2,1)} %get-tuple-element.33., ...), custom_call_target="tpu_custom_call" | custom-call | tf_op jit(solution)/shard_map/finish/pallas_call | solution.py:556

commit v7 on v6

--- a/solution.py
+++ b/solution.py
@@ -14,6 +14,7 @@
 MESH = pl.DeviceIdType.MESH
 TILE = 1024
 VMEM_LIMIT = 60 * 1024 * 1024
+STEP_LIMIT = 56 * 1024 * 1024
 
 
 def nn(lhs, rhs):
@@ -476,31 +477,34 @@
     for g, k in ((4, 1), (5, 1), (1, 7), (4, 2), (5, 2), (2, 4), (3, 4), (1, 8), (4, 3), (5, 3), (2, 5), (3, 5), (4, 4), (5, 4), (2, 6), (3, 6),
                  (4, 5), (5, 5), (2, 7), (3, 7), (4, 6), (5, 6), (2, 8), (3, 8)):
         red[g].step(k)()
-    puts = [(r_weu, 3 * lat, d_weu), (r_wmu, 2 * lat, d_wmu), (r_wgu, lat, d_wgu), (r_two1, lat, d_two.at[1]),
-            (r_two2, lat, d_two.at[2]), (r_two3, lat, d_two.at[3]), (r_two4, lat, d_two.at[4]), (r_two5, lat, d_two.at[5])]
-    moves = [pltpu.make_async_copy(out.at[pl.ds(a, n)], ref, out_sem.at[3 + k]) for k, (a, n, ref) in enumerate(puts)]
-    for move in moves:
-        move.start()
+    puts = [(r_weu, 3 * lat, d_weu), (r_wmu, 2 * lat, d_wmu), (r_wgu, lat, d_wgu)]
+    twos = [r_two0, r_two1, r_two2, r_two3, r_two4, r_two5]
+    for row, n, ref in puts:
+        ref[...] = out[row:row + n, :]
+    for k in range(1, 6):
+        d_two[k] = out[twos[k]:twos[k] + lat, :]
     for k in range(7, 9):
         red[4].step(k)()
         red[5].step(k)()
-    last = pltpu.make_async_copy(out.at[pl.ds(r_two0, lat)], d_two.at[0], out_sem.at[11])
-    last.start()
+    d_two[0] = out[twos[0]:twos[0] + lat, :]
     d_wgi[...] = out[r_wgi:r_wgi + n_feat, :]
     d_wmi[...] = out[r_wmi:r_wmi + 3, :]
     d_wei[...] = out[r_wei:r_wei + 4, :]
     for k in range(6):
         d_vec_out[k] = out[r_vec + 4 * k:r_vec + 4 * k + 4, :]
-    for copy in stores + moves + [last]:
+    for copy in stores:
         copy.wait()
 
 
 def finish_kernel(*refs):
     n = (len(refs) - 2) // 3
     srcs, dsts, held, (in_sem, out_sem) = refs[:n], refs[n:2 * n], refs[2 * n:3 * n], refs[3 * n:]
-    takes = [pltpu.make_async_copy(srcs[k], held[k], in_sem.at[k]) for k in range(n)]
-    gives = [pltpu.make_async_copy(held[k], dsts[k], out_sem.at[k]) for k in range(n)]
+    big = 3
+    takes = [pltpu.make_async_copy(srcs[k], held[k], in_sem.at[k]) for k in range(big)]
+    gives = [pltpu.make_async_copy(held[k] if k < big else srcs[k], dsts[k], out_sem.at[k]) for k in range(n)]
     for copy in takes:
+        copy.start()
+    for copy in gives[big:]:
         copy.start()
     for take, give in zip(takes, gives):
         take.wait()
@@ -532,7 +536,7 @@
             return jax.ShapeDtypeStruct(shape, dtype)
         outs = [sds((n_mesh, lat), BF), sds((n_grid, lat), BF), sds((n_feat, n_grid), F32), sds(w_grid_in.shape, F32), sds(w_mesh_in.shape, F32), sds(w_edge_in.shape, F32),
                 sds(w_edge_up.shape, F32), sds(w_mesh_up.shape, F32), sds(w_grid_up.shape, F32), sds(w_second.shape, F32), sds(vectors.shape, F32)]
-        out_specs = [far, far, far, near, near, near, far, far, far, far, near]
+        out_specs = [far] * 3 + [near] * 8
         V = pltpu.VMEM
         D = pltpu.SemaphoreType.DMA
         scratch = [V(w_edge_up.shape, BF), V(w_mesh_up.shape, BF), V(w_grid_up.shape, BF), V((n_mesh, lat), BF), V((n_grid, lat), BF),
@@ -549,7 +553,7 @@
             in_specs=[near] * 11 + [far] * 5,
             out_specs=out_specs,
             scratch_shapes=scratch,
-            compiler_params=pltpu.CompilerParams(vmem_limit_bytes=VMEM_LIMIT, collective_id=0, has_side_effects=True),
+            compiler_params=pltpu.CompilerParams(vmem_limit_bytes=STEP_LIMIT, collective_id=0, has_side_effects=True),
             name='step',
         )(grid_in.T, mesh_static.T, edge_static.T, send_rows, edge_src.reshape(-1, 128), edge_dst.reshape(-1, 128),
           w_grid_in, w_mesh_in, w_edge_in, w_second, vectors, w_edge_up, w_mesh_up, w_grid_up, d_mesh_out, d_grid_out)

time: 144 us -> 241 us (1.67)
  Pallas kernels: 143 us -> 240 us
    pallas_call x1, Pallas kernels: 6.21 us -> 103 us  [local_step(): pl.pallas_call(finish_kernel, out_shape=outs, in_specs=[far] * len(outs),...]
where the time goes in v7:
time: 241 us
  Pallas kernels  240 us (100%)
    pallas_call x1, Pallas kernels, local_step(): pl.pallas_call(functools.partial(step_kernel, parts), out_shape=outs, in_...  137 us
    pallas_call x1, Pallas kernels, local_step(): pl.pallas_call(finish_kernel, out_shape=outs, in_specs=[far] * len(outs),...  103 us

profile of v7, /device:TPU:0, one launch (start us, length us, event | category | flops | bytes accessed | tf_op | source)
XLA Modules:
  0.0 240.8 jit_solution(15720975307202329711)
XLA Ops:
  0.7 137.1 %step.1 = (bf16[2048,256]{1,0:T(8,128)(2,1)}, bf16[2048,256]{1,0:T(8,128)(2,1)}, f32[164,2048]{1,0:T(8,128)}, f32[164,256]{1,0:T(8,128)}, f32[3,256]{1,0:T(4,128...) custom-call(bf16[164,2048]{1,0:T(8,128)(2,1)} %bitcast.6, ...), custom_call_target="tpu_custom_call" | custom-call | tf_op jit(solution)/shard_map/step/pallas_call | solution.py:550
  137.8 102.8 %finish.1 = (bf16[2048,256]{1,0:T(8,128)(2,1)}, bf16[2048,256]{1,0:T(8,128)(2,1)}, f32[164,2048]{1,0:T(8,128)}, f32[164,256]{1,0:T(8,128)}, f32[3,256]{1,0:T(4,1...) custom-call(bf16[2048,256]{1,0:T(8,128)(2,1)} %get-tuple-element.33., ...), custom_call_target="tpu_custom_call" | custom-call | tf_op jit(solution)/shard_map/finish/pallas_call | solution.py:560
